TPU v7x, 256 devices: a whole 4x4x8 slice. The times are simulated.
256 devices in a mesh: rows: 256 (over y, x, z, core).
Axes of the slice: x: 4, y: 4, z: 8, core: 2. Of those that a mesh axis runs over, the one named last changes fastest.
Arguments:
- source: float32 [64, 1048576], P(None, 'rows'), may hold values from -6 to 6
- band_values: float32 [128, 1048576], P(None, 'rows'), may hold values from -0.625 to 0.625
- offsets: int32 [128], replicated, may hold values from -128 to 128, as said below
Outputs:
- compressed: float32 [128, 1048576], P(None, 'rows')
Inputs may be any that keep to these rules, and one draw needn't show every extreme that they name: The 128 offsets are distinct and include both -128 and 128.
All inputs are finite; a program needn't handle non-finite values.
Results may differ from a plain program's by a relative error of at most 0.0003.
Values sent between devices are 32-bit elements; how exact they have to be, the bound alone decides.
No kernel may reach another device: no remote copies, remote signals or barrier semaphores. Data moves between devices by JAX's collectives and lax.ppermute only.
A program may use at most 192 MiB of HBM per device.

v0:
```python
import jax
import jax.numpy as jnp
import numpy as np
from jax import lax
from jax.sharding import Mesh
from jax.sharding import PartitionSpec as P

HB = 128
K2 = 128
ROWS = ("rows_0", "rows_1", "rows_2", "rows_3")


def copy_for_each(x, axis):
    copies = jnp.broadcast_to(x, (lax.axis_size(axis), *x.shape))
    return lax.all_to_all(copies, axis, split_axis=0, concat_axis=0, tiled=True)


def taken_together(x, axis):
    return copy_for_each(x, axis).sum(axis=0)


def by_axis(x, axes):
    far, near = axes
    nearer = taken_together(x, near)
    return taken_together(nearer, far)


def rows_for(lines, devices):
    spare = -len(lines) % devices
    return jnp.pad(lines, [(0, spare)] + [(0, 0)] * (lines.ndim - 1))


def laid_out(blocks, dim):
    lengths = list(blocks.shape[1:])
    lengths[dim] *= blocks.shape[0]
    return jnp.moveaxis(blocks, 0, dim).reshape(lengths)


def whole_of(x, axes, dim):
    far, near = axes
    leading = copy_for_each(x, far)
    blocks = jnp.swapaxes(copy_for_each(leading, near), 0, 1)
    return laid_out(blocks.reshape(-1, *x.shape), dim)


def in_blocks(x, dim, devices):
    lengths = x.shape
    blocks = x.reshape(*lengths[:dim], devices, lengths[dim] // devices, *lengths[dim + 1 :])
    return jnp.moveaxis(blocks, dim, 0)


def summed_on_arrival(x, axis, dim):
    devices = lax.axis_size(axis)
    blocks = lax.all_to_all(in_blocks(x, dim, devices), axis, 0, 0, tiled=True)
    return jnp.sum(blocks, axis=0)


def sum_in_two_steps(x, axes, dim):
    far, near = axes
    blocks = in_blocks(x, dim, lax.axis_size(far))
    nearer = summed_on_arrival(blocks, near, dim + 1)
    arrived = lax.all_to_all(nearer, far, split_axis=0, concat_axis=0, tiled=True)
    return arrived.sum(axis=0)


def sum_by_parts(x, axes):
    padded = rows_for(x, lax.axis_size(axes[0]) * lax.axis_size(axes[1]))
    whole = whole_of(sum_in_two_steps(padded, axes, 0), axes, 0)
    return lax.slice_in_dim(whole, 0, len(x)).reshape(x.shape)


def packed_total_2(arrays, axis):
    ends = [0]
    for a in arrays:
        ends.append(ends[-1] + a.size)
    total = sum_by_parts(jnp.concatenate([a.ravel() for a in arrays]), axis)
    return tuple((total[b:e].reshape(a.shape) for a, b, e in zip(arrays, ends, ends[1:])))


def padded(block, sides, width, periodic):
    for axis, dim in sides:
        count = lax.axis_size(axis)
        forward = [(i, i + 1) for i in range(count - 1)]
        if periodic:
            forward.append((count - 1, 0))
        backward = [(target, source) for source, target in forward]
        low = lax.ppermute(
            lax.slice_in_dim(block, block.shape[dim] - width, None, axis=dim), axis, forward
        )
        high = lax.ppermute(lax.slice_in_dim(block, 0, width, axis=dim), axis, backward)
        block = jnp.concatenate([low, block, high], axis=dim)
    return block


def band_blocks(band_values, offsets):
    diagonals = band_values.shape[0]
    blocks = band_values.shape[1] // HB
    values = band_values.reshape(diagonals, blocks, HB).transpose(1, 0, 2)
    within = jnp.arange(HB, dtype=jnp.int32)
    columns = within[None, :] + offsets[:, None] + HB
    row_index = jnp.broadcast_to(within[None, :], columns.shape)
    blocked = jnp.zeros((blocks, HB, 3 * HB), values.dtype)
    return blocked.at[:, row_index, columns].set(values)


def apply_band(extended, blocked):
    width = extended.shape[0]
    blocks = blocked.shape[0]
    pieces = extended.reshape(width, blocks + 2, HB)
    windows = jnp.concatenate([pieces[:, :-2], pieces[:, 1:-1], pieces[:, 2:]], axis=2)
    result = jnp.einsum("cbj,brj->cbr", windows, blocked, precision=lax.Precision.HIGHEST)
    return result.reshape(width, blocks * HB)


def compress(grammian, retain):
    spanning = grammian[:, :retain]
    coeffs = None
    for repeat in range(2):
        if repeat > 0:
            spanning = jnp.dot(grammian, coeffs.T, precision=lax.Precision.HIGHEST)
        mapped = jnp.dot(grammian, spanning, precision=lax.Precision.HIGHEST)
        metric = jnp.dot(spanning.T, mapped, precision=lax.Precision.HIGHEST)
        metric = 0.5 * (metric + metric.T)
        factor = jnp.linalg.cholesky(metric)
        coeffs = jax.scipy.linalg.solve_triangular(factor, spanning.T, lower=True)
    return coeffs


def pack_upper(square):
    upper_rows, upper_cols = np.triu_indices(square.shape[0])
    return square[upper_rows, upper_cols]


def unpack_upper(packed, order):
    upper_rows, upper_cols = np.triu_indices(order)
    upper = jnp.zeros((order, order), jnp.float32).at[upper_rows, upper_cols].set(packed)
    return upper + jnp.triu(upper, 1).T


def first_gram(first, total):
    local = jnp.dot(first, first.T, precision=lax.Precision.HIGHEST)
    packed_total = by_axis(pack_upper(local), (("rows_0", "rows_1"), ("rows_2", "rows_3")))
    return unpack_upper(packed_total, local.shape[0]) / total


def second_gram(factor, squared, coeffs_one, gram_one, total):
    known = jnp.dot(
        jnp.dot(coeffs_one, gram_one, precision=lax.Precision.HIGHEST),
        coeffs_one.T,
        precision=lax.Precision.HIGHEST,
    )
    cross = jnp.dot(factor, squared.T, precision=lax.Precision.HIGHEST)
    tail = jnp.dot(squared, squared.T, precision=lax.Precision.HIGHEST)
    cross_total, tail_total = packed_total_2(
        (cross, pack_upper(tail)), ("rows_0", ("rows_1", "rows_2", "rows_3"))
    )
    cross_total = cross_total / total
    tail_full = unpack_upper(tail_total, squared.shape[0]) / total
    top = jnp.concatenate([known, cross_total], axis=1)
    bottom = jnp.concatenate([cross_total.T, tail_full], axis=1)
    return jnp.concatenate([top, bottom], axis=0)


def reach_out(factor):
    return padded(factor, ((ROWS, 1),), HB, False)


def body(source, band_values, offsets):
    devices_here = lax.axis_size(ROWS)
    total = float(source.shape[1] * devices_here)
    keep_first = 2 * source.shape[0]
    blocked = band_blocks(band_values, offsets)
    extended = padded(source, ((ROWS, 1),), HB, False)
    first = jnp.concatenate([source, apply_band(extended, blocked)], axis=0)
    gram_one = first_gram(first, total)
    coeffs_one = compress(gram_one, keep_first)
    factor = jnp.dot(coeffs_one, first, precision=lax.Precision.HIGHEST)
    once_more = apply_band(reach_out(factor), blocked)
    squared = apply_band(reach_out(once_more), blocked)
    second = jnp.concatenate([factor, squared], axis=0)
    coeffs_two = compress(second_gram(factor, squared, coeffs_one, gram_one, total), K2)
    return jnp.dot(coeffs_two, second, precision=lax.Precision.HIGHEST)


def solution(mesh):
    torus = Mesh(mesh.devices.reshape(4, 4, 8, 2), ("rows_0", "rows_1", "rows_2", "rows_3"))
    in_specs = (P(None, ROWS), P(None, ROWS), P())
    out_specs = P(None, ROWS)
    return jax.shard_map(body, mesh=torus, in_specs=in_specs, out_specs=out_specs, check_vma=False)
```

profile of v0, /device:TPU:1, one launch (start us, length us, event | category | flops | bytes accessed | tf_op | source)
XLA Modules:
  0.0 564.9 jit_solution(9466394486775668503)
XLA Ops:
  15.5 50.8 %scatter_custom_fusion = f32[32,49152]{0,1:T(8,128)} fusion(s32[16384]{0:T(1024)S(1)} %select_bitcast_fusion, f32[16384,32]{1,0:T(8,128)} %bitcast.149, f32[]{:T(128)} %constant.61.clone.1), kind=kCustom, calls=%fused_computation.5 | custom fusion | bytes 6291968
  66.2 17.2 %copy.173 = f32[32,128,384]{2,1,0:T(8,128)} copy(f32[32,128,384]{0,2,1:T(8,128)} %bitcast.142) | data formatting | bytes 12582912 | tf_op jit(solution)/shard_map/scatter | solution.py:103
  88.4 8.9 %fusion.26 = f32[32,8,8,128]{3,2,1,0:T(8,128)S(1)} fusion(f32[32,128,384]{2,1,0:T(8,128)S(1)} %bitcast.141, f32[64,32,128]{2,0,1:T(8,128)S(1)} %copy.211, f32[64,32,128]{2,0,1:T(8,128)S(1)} %copy.210, f32[64,32,128]{2,0,1:T(8,128)S(1)} %copy.209), kind=kOutput, calls=%fused_computation.34 | convolution fusion | flops 1209532416 | bytes 10485760 | tf_op jit(solution)/shard_map/cbj,brj->cbr/dot_general | solution.py:111
  100.5 48.0 %gather_fusion = f32[8256]{0:T(1024)S(1)} fusion(f32[128,128]{1,0:T(8,128)S(1)} %fusion.88, s32[8256]{0:T(1024)S(1)} %copy-done), kind=kCustom, calls=%fused_computation | custom fusion | bytes 132096 | tf_op jit(solution)/shard_map/gather | solution.py:131
  148.8 27.5 %all_to_all.40 = f32[16,1,8256]{2,1,0:T(1,128)S(1)} all-to-all(f32[16,1,8256]{2,1,0:T(1,128)S(1)} %broadcast_in_dim.62), channel_id=1, replica_groups=mesh['rows_0'=4,'rows_1'=4,'rows_2'=8,'rows_3'=2] {'rows_2','rows_3'}, dimensions={0} | all-to-all | bytes 1056768 | tf_op jit(solution)/shard_map/all_to_all | solution.py:15
  176.9 17.6 %all_to_all.41 = f32[16,1,8256]{2,1,0:T(1,128)S(1)} all-to-all(f32[16,1,8256]{2,1,0:T(1,128)S(1)} %broadcast_in_dim.63), channel_id=1, replica_groups=mesh['rows_0'=4,'rows_1'=4,'rows_2'=8,'rows_3'=2] {'rows_0','rows_1'}, dimensions={0} | all-to-all | bytes 1056768 | tf_op jit(solution)/shard_map/all_to_all | solution.py:15
  194.9 40.0 %scatter_custom_fusion.1 = f32[16384]{0:T(1024)S(1)} fusion(s32[8256]{0:T(1024)} %constant.105, f32[8256]{0:T(1024)S(1)} %reduce_sum.37, f32[]{:T(128)} %constant.61.clone.1), kind=kCustom, calls=%fused_computation.103 | custom fusion | bytes 66048
  235.7 11.7 %cholesky.74 = f32[128,128]{1,0:T(8,128)S(1)} custom-call(f32[128,128]{1,0:T(8,128)S(1)} %fusion.55), custom_call_target="Cholesky" | custom-call | tf_op jit(solution)/shard_map/jit(cholesky)/cholesky | solution.py:124
  248.9 9.8 %custom-call.14 = f32[1,128,128]{1,2,0:T(8,128)S(1)} custom-call(f32[1,128,128]{2,1,0:T(8,128)S(1)} %fusion.36), custom_call_target="InvertDiagBlocksLowerTriangular" | custom-call | tf_op jit(solution)/shard_map/jit(_solve_triangular)/triangular_solve | solution.py:125
  260.1 11.7 %cholesky.85 = f32[128,128]{1,0:T(8,128)S(1)} custom-call(f32[128,128]{1,0:T(8,128)S(1)} %fusion.50), custom_call_target="Cholesky" | custom-call | tf_op jit(solution)/shard_map/jit(cholesky)/cholesky | solution.py:124
  273.3 10.0 %custom-call.15 = f32[1,128,128]{1,2,0:T(8,128)S(1)} custom-call(f32[1,128,128]{2,1,0:T(8,128)S(1)} %fusion.37), custom_call_target="InvertDiagBlocksLowerTriangular" | custom-call | tf_op jit(solution)/shard_map/jit(_solve_triangular)/triangular_solve | solution.py:125
  301.0 5.8 %fusion.83 = (f32[128,32,128]{0,2,1:T(8,128)}, f32[128,32,128]{0,2,1:T(8,128)}, f32[128,32,128]{0,2,1:T(8,128)}) fusion(f32[128,34,128]{0,2,1:T(8,128)} %bitcast.146), kind=kLoop, calls=%fused_computation.121 | loop fusion | bytes 12582912 | tf_op jit(solution)/shard_map/slice | solution.py:110
  315.6 10.9 %fusion.2 = f32[32,128,128]{2,1,0:T(8,128)S(1)} fusion(f32[32,128,384]{2,1,0:T(8,128)} %copy.173, f32[128,32,128]{2,0,1:T(8,128)} %copy.214, f32[128,32,128]{2,0,1:T(8,128)} %copy.213, f32[128,32,128]{2,0,1:T(8,128)} %copy.212), kind=kOutput, calls=%fused_computation.7 | convolution fusion | flops 2419064832 | bytes 14680064 | tf_op jit(solution)/shard_map/cbj,brj->cbr/dot_general | solution.py:111
  345.7 10.9 %fusion.8 = f32[32,128,128]{2,1,0:T(8,128)S(1)} fusion(f32[32,128,384]{2,1,0:T(8,128)} %copy.173, f32[128,32,128]{2,0,1:T(8,128)} %copy.217, f32[128,32,128]{2,0,1:T(8,128)} %copy.216, f32[128,32,128]{2,0,1:T(8,128)} %copy.215), kind=kOutput, calls=%fused_computation.13 | convolution fusion | flops 2419064832 | bytes 14680064 | tf_op jit(solution)/shard_map/cbj,brj->cbr/dot_general | solution.py:111
  362.4 48.0 %gather_fusion.1 = f32[8256]{0:T(1024)S(1)} fusion(f32[128,128]{1,0:T(8,128)S(1)} %fusion.29, s32[8256]{0:T(1024)S(1)} %copy-done), kind=kCustom, calls=%fused_computation.1 | custom fusion | bytes 132096 | tf_op jit(solution)/shard_map/gather | solution.py:131
  410.8 25.3 %all_to_all.42 = f32[64,4,97]{2,1,0:T(4,128)S(1)} all-to-all(f32[64,4,97]{2,1,0:T(4,128)S(1)} %copy.194), channel_id=1, replica_groups=mesh['rows_0'=4,'rows_1'=4,'rows_2'=8,'rows_3'=2] {'rows_1','rows_2','ro..., dimensions={0} | all-to-all | bytes 198656 | tf_op jit(solution)/shard_map/all_to_all | solution.py:54
  436.2 7.0 %all_to_all.43 = f32[4,1,97]{2,1,0:T(1,128)S(1)} all-to-all(f32[4,1,97]{2,1,0:T(1,128)S(1)} %bitcast.157), channel_id=1, replica_groups=mesh['rows_0'=4,'rows_1'=4,'rows_2'=8,'rows_3'=2] {'rows_0'}, dimensions={0} | all-to-all | bytes 3104 | tf_op jit(solution)/shard_map/all_to_all | solution.py:62
  451.8 7.3 %all-to-all-start.5 = ((f32[64,4,97]{2,1,0:T(4,128)}), f32[64,4,97]{2,1,0:T(4,128)S(1)}, u32[]{:S(2)}, u32[]{:S(2)}) async-start(f32[64,4,97]{2,1,0:T(4,128)} %broadcast_in_dim.67), calls=%async_computation.5 | async-start | bytes 262144 | tf_op jit(solution)/shard_map/all_to_all | solution.py:15
  462.3 7.2 %all-to-all-done.5 = f32[64,4,97]{2,1,0:T(4,128)S(1)} async-done(((f32[64,4,97]{2,1,0:T(4,128)}), f32[64,4,97]{2,1,0:T(4,128)S(1)}, u32[]{:S(2)}, u32[]{:S(2)}) %all-to-all-start.5) | async-done | bytes 99360 | tf_op jit(solution)/shard_map/all_to_all | solution.py:15
  469.9 39.7 %scatter_custom_fusion.2 = f32[16384]{0:T(1024)S(1)} fusion(s32[8256]{0:T(1024)} %constant.105, f32[8256]{0:T(1024)S(1)} %slice.109, f32[]{:T(128)} %constant.61.clone.1), kind=kCustom, calls=%fused_computation.101 | custom fusion | bytes 66048
  511.1 11.7 %cholesky.96 = f32[128,128]{1,0:T(8,128)S(1)} custom-call(f32[128,128]{1,0:T(8,128)S(1)} %fusion.44), custom_call_target="Cholesky" | custom-call | tf_op jit(solution)/shard_map/jit(cholesky)/cholesky | solution.py:124
  524.1 9.8 %custom-call.16 = f32[1,128,128]{1,2,0:T(8,128)S(1)} custom-call(f32[1,128,128]{2,1,0:T(8,128)S(1)} %fusion.38), custom_call_target="InvertDiagBlocksLowerTriangular" | custom-call | tf_op jit(solution)/shard_map/jit(_solve_triangular)/triangular_solve | solution.py:125
  536.1 11.9 %cholesky.107 = f32[128,128]{1,0:T(8,128)S(1)} custom-call(f32[128,128]{1,0:T(8,128)S(1)} %fusion.41), custom_call_target="Cholesky" | custom-call | tf_op jit(solution)/shard_map/jit(cholesky)/cholesky | solution.py:124
  549.3 9.8 %custom-call.17 = f32[1,128,128]{1,2,0:T(8,128)S(1)} custom-call(f32[1,128,128]{2,1,0:T(8,128)S(1)} %fusion.39), custom_call_target="InvertDiagBlocksLowerTriangular" | custom-call | tf_op jit(solution)/shard_map/jit(_solve_triangular)/triangular_solve | solution.py:125
  (137 shorter events, 105.4 us)
Async XLA Ops:
  0.0 10.2 %copy-start.7 = (s32[2]{0:T(128)S(1)}, s32[2]{0:T(128)}, u32[]{:S(2)}) copy-start(s32[2]{0:T(128)} %constant.72) | copy-start | bytes 28
  0.0 10.3 %copy-start.8 = (s32[2]{0:T(128)S(1)}, s32[2]{0:T(128)}, u32[]{:S(2)}) copy-start(s32[2]{0:T(128)} %constant.75) | copy-start | bytes 28
  0.0 10.1 %copy-start.6 = (s32[128]{0:T(128)S(1)}, s32[128]{0:T(128)}, u32[]{:S(2)}) copy-start(s32[128]{0:T(128)} %param.26) | copy-start | bytes 1540
  0.0 10.4 %copy-start.5 = (f32[128,4096]{1,0:T(8,128)S(1)}, f32[128,4096]{1,0:T(8,128)}, u32[]{:S(2)}) copy-start(f32[128,4096]{1,0:T(8,128)} %param.25) | copy-start | bytes 6291460
  1.0 82.5 %collective-permute-start = (f32[64,128]{1,0:T(8,128)S(1)}, f32[64,128]{1,0:T(8,128)S(1)}, u32[]{:S(2)}, u32[]{:S(2)}) collective-permute-start(f32[64,128]{1,0:T(8,128)S(1)} %get-tuple-element.21), channel_id=1, source_target_pairs={{0,1},{1,2},{2,3},{3,4},{4,5},{5,6},{6,7},{7,8},{8,9},{9,10},{10,1... | collective-permute-start | bytes 98312 | tf_op jit(solution)/shard_map/ppermute | solution.py:87
  5.9 77.6 %collective-permute-start.1 = (f32[64,128]{1,0:T(8,128)S(1)}, f32[64,128]{1,0:T(8,128)S(1)}, u32[]{:S(2)}, u32[]{:S(2)}) collective-permute-start(f32[64,128]{1,0:T(8,128)S(1)} %get-tuple-element.22), channel_id=1, source_target_pairs={{1,0},{2,1},{3,2},{4,3},{5,4},{6,5},{7,6},{8,7},{9,8},{10,9},{11,1... | collective-permute-start | bytes 98312 | tf_op jit(solution)/shard_map/ppermute | solution.py:90
  66.2 17.2 %copy-start.4 = (f32[64,4096]{1,0:T(8,128)S(1)}, f32[64,4096]{1,0:T(8,128)}, u32[]{:S(2)}) copy-start(f32[64,4096]{1,0:T(8,128)} %param.24) | copy-start | bytes 3145732
  84.5 3.8 slice-start
  86.1 2.3 slice-start.1
  88.4 8.9 %copy-start.2 = (f32[128,4096]{1,0:T(8,128)S(1)}, f32[128,4096]{1,0:T(8,128)}, u32[]{:S(2)}) copy-start(f32[128,4096]{1,0:T(8,128)} %constant_dynamic-update-slice_fusion) | copy-start | bytes 6291460
  97.3 1.3 copy-start.3
  98.7 1.8 copy-start
  287.0 5.8 %collective-permute-start.2 = (f32[128,128]{1,0:T(8,128)S(1)}, f32[128,128]{1,0:T(8,128)S(1)}, u32[]{:S(2)}, u32[]{:S(2)}) collective-permute-start(f32[128,128]{1,0:T(8,128)S(1)} %get-tuple-element.16), channel_id=1, source_target_pairs={{0,1},{1,2},{2,3},{3,4},{4,5},{5,6},{6,7},{7,8},{8,9},{9,10},{10,1... | collective-permute-start | bytes 196616 | tf_op jit(solution)/shard_map/ppermute | solution.py:87
  290.9 5.6 collective-permute-start.3
  326.5 4.7 collective-permute-start.4
  328.4 5.6 collective-permute-start.5
  356.6 3.6 copy-start.1
  443.8 7.4 %all-to-all-start.4 = ((f32[4,1,97]{2,1,0:T(1,128)}), f32[4,1,97]{2,1,0:T(1,128)S(1)}, u32[]{:S(2)}, u32[]{:S(2)}) async-start(f32[4,1,97]{2,1,0:T(1,128)} %broadcast_in_dim.66), calls=%async_computation.4 | async-start | bytes 4096 | tf_op jit(solution)/shard_map/all_to_all | solution.py:15
  451.8 17.6 %all-to-all-start.5 = ((f32[64,4,97]{2,1,0:T(4,128)}), f32[64,4,97]{2,1,0:T(4,128)S(1)}, u32[]{:S(2)}, u32[]{:S(2)}) async-start(f32[64,4,97]{2,1,0:T(4,128)} %broadcast_in_dim.67), calls=%async_computation.5 | async-start | bytes 262144 | tf_op jit(solution)/shard_map/all_to_all | solution.py:15
where the time goes:
time: 571 us; the launch traced here: 565 us
  local copies, waits for them, and re-layouts  293 us (51%)
  other arithmetic  95.9 us (17%)
  blocking collectives  77.4 us (14%)
  matrix products  52.3 us (9%)
  starting transfers between devices  27.9 us (5%)
  waiting for transfers between devices  17.4 us (3%)
    unnamed x37, local copies, waits for them, and re-layouts  154 us
    gather x2, local copies, waits for them, and re-layouts, pack_upper(): return square[upper_rows, upper_cols]  96.1 us
    another operation x12, other arithmetic, compress(): factor = jnp.linalg.cholesky(metric)  49.9 us
    all_to_all x2, blocking collectives, copy_for_each(): return lax.all_to_all(copies, axis, split_axis=0, concat_axis=0, tiled=True)  45.1 us
    another operation x8, other arithmetic, compress(): coeffs = jax.scipy.linalg.solve_triangular(factor, spanning.T, lower=True)  42.1 us
    dot_general x3, matrix products, apply_band(): jnp.einsum('cbj,brj->cbr', windows, blocked, precision=lax.Precision.HIGH...  30.7 us
    all_to_all x1, blocking collectives, summed_on_arrival(): blocks = lax.all_to_all(in_blocks(x, dim, devices), axis, 0, 0, tiled=True)  25.3 us
    scatter x1, local copies, waits for them, and re-layouts, band_blocks(): return blocked.at[:, row_index, columns].set(values)  17.2 us
  transfers between devices with their start and end apart: 8, of which 4 were waited for; matrix products, arithmetic and copies ran while one was open for 14% of the time, Pallas kernels for 0%

commit v1 on v0

v1 whole, which is shorter than its diff:
```python
import functools

import jax
import jax.numpy as jnp
from jax import lax
from jax.experimental import pallas as pl
from jax.experimental.pallas import tpu as pltpu
from jax.sharding import PartitionSpec as P

HB = 128
WB = 256
NT = (((1,), (1,)), ((), ()))
TN = (((0,), (0,)), ((), ()))


def split(x):
    high = x.astype(jnp.bfloat16)
    return high, (x - high.astype(jnp.float32)).astype(jnp.bfloat16)


def mm(a, b, dims=(((1,), (0,)), ((), ()))):
    return lax.dot_general(a, b, dims, preferred_element_type=jnp.float32)


def exact(a, b, dims=(((1,), (0,)), ((), ()))):
    return lax.dot_general(
        a, b, dims, precision=lax.Precision.HIGHEST, preferred_element_type=jnp.float32
    )


def powers_kernel(total, src_ref, band_ref, off_ref, high_ref, low_ref, gram_ref, xh, xl, wh, wl):
    rows = src_ref.shape[0]
    width = high_ref.shape[1]
    blocks = width // WB + 2
    diagonals = off_ref.shape[0]
    span = 2 * WB
    lanes = lax.broadcasted_iota(jnp.int32, (diagonals, span), 1)
    pick = jnp.where(lanes == off_ref[...] + HB, 1.0, 0.0).astype(jnp.bfloat16)
    pick = jnp.concatenate([pick, pick], axis=0)

    high, low = split(src_ref[...])
    xh[0], xl[0] = high, low
    edge = jnp.zeros((rows, HB), jnp.bfloat16)
    for power in (1, 2):
        for buf in (xh, xl):
            buf[power, :, :HB] = edge
            buf[power, :, buf.shape[2] - HB :] = edge

    def build(b, _):
        at = pl.multiple_of(b * WB, WB)
        vh, vl = split(band_ref[:, pl.ds(at, WB)])
        both = jnp.concatenate([vh, vl], axis=0)
        diag = mm(both, pick, TN)
        band = pltpu.roll(diag, 0, 1, stride=1, stride_axis=0)
        wh[b], wl[b] = split(band)
        return 0

    lax.fori_loop(0, blocks, build, 0)

    def apply(power, b):
        at = pl.multiple_of(b * WB, WB)
        window = pl.ds(at, span)
        left_h = xh[power - 1, :, window]
        both = jnp.concatenate([left_h, xl[power - 1, :, window]], axis=0)
        by_high = mm(both, wh[b], NT)
        return by_high[:rows] + by_high[rows:] + mm(left_h, wl[b], NT)

    for power in (1, 2):

        def step(b, _):
            h, l = split(apply(power, b))
            place = pl.ds(pl.multiple_of(b * WB + HB, HB), WB)
            xh[power, :, place] = h
            xl[power, :, place] = l
            return 0

        lax.fori_loop(0, blocks, step, 0)

    for power in range(3):
        high_ref[power * rows : (power + 1) * rows, :] = xh[power, :, 3 * HB : 3 * HB + width]
        low_ref[power * rows : (power + 1) * rows, :] = xl[power, :, 3 * HB : 3 * HB + width]

    def last(b, acc):
        h, l = split(apply(3, b + 1))
        place = pl.ds(pl.multiple_of(b * WB, WB), WB)
        high_ref[3 * rows :, place] = h
        low_ref[3 * rows :, place] = l
        tall = high_ref[:, place]
        return acc + mm(tall, tall, NT) + 2.0 * mm(tall, low_ref[:, place], NT)

    gram = lax.fori_loop(0, blocks - 2, last, jnp.zeros((4 * rows, 4 * rows), jnp.float32))
    gram = (gram + gram.T) * (0.5 / total)
    half = gram.shape[1] // 2
    gram_ref[0] = gram[:, :half]
    gram_ref[1] = gram[:, half:]


def lane_copy(x, lane):
    return jnp.broadcast_to(x[:, lane : lane + 1], (8, 128))


def row_copy(x, row):
    return jnp.broadcast_to(x[row : row + 1, :], (8, 128))


def eliminate(work, tiles):
    order = work.shape[0]
    sub = lax.broadcasted_iota(jnp.int32, (8, 128), 0)

    def tile(g, t):
        return slice(8 * g, 8 * g + 8), slice(128 * t, 128 * t + 128)

    for kb in range(order // 8):
        own = [work[tile(kb, t)] for t in range(tiles)]
        cols = [lane_copy(own[0], 8 * kb + j) for j in range(8)]
        inverses, cross, tops = [], [], []
        pivots = jnp.ones((8, 128), jnp.float32)
        for k in range(8):
            pivot = row_copy(cols[k], k)
            inverse = 1.0 / pivot
            pivots = jnp.where(sub == k, pivot, pivots)
            m = jnp.where(sub > k, cols[k] * inverse, 0.0)
            crossing = [row_copy(cols[j], k) for j in range(k + 1, 8)]
            top = [row_copy(x, k) for x in own]
            for j in range(k + 1, 8):
                cols[j] = cols[j] - m * crossing[j - k - 1]
            own = [x - m * y for x, y in zip(own, top)]
            inverses.append(inverse)
            cross.append(crossing)
            tops.append(top)
        scale = lax.rsqrt(pivots)
        for t in range(1, tiles):
            work[tile(kb, t)] = own[t] * scale
        for g in range(kb + 1, order // 8):
            rest = [work[tile(g, t)] for t in range(tiles)]
            q = [lane_copy(rest[0], 8 * kb + j) for j in range(8)]
            for k in range(8):
                m = q[k] * inverses[k]
                for j in range(k + 1, 8):
                    q[j] = q[j] - m * cross[k][j - k - 1]
                rest = [x - m * y for x, y in zip(rest, tops[k])]
            for t in range(tiles):
                work[tile(g, t)] = rest[t]


def compress(gram, retain, work):
    order = gram.shape[0]
    spanning = gram[:retain]
    for turn in range(2):
        if turn > 0:
            spanning = exact(work[:, retain : retain + order], gram)
        mapped = exact(spanning, gram)
        metric = exact(mapped, spanning, NT)
        work[:, :retain] = 0.5 * (metric + metric.T)
        work[:, retain : retain + order] = spanning
        eliminate(work, (retain + order) // 128)
    return work[:, retain : retain + order]


def finish_kernel(gram_ref, high_ref, low_ref, out_ref, work):
    keep = out_ref.shape[0]
    g11 = gram_ref[0, :keep]
    g12 = gram_ref[1, :keep]
    g22 = gram_ref[1, keep:]
    one = compress(g11, keep, work)
    mixed = [exact(exact(one, g), one, NT) for g in (g11, g12, g22)]
    top = jnp.concatenate([mixed[0], mixed[1]], axis=1)
    bottom = jnp.concatenate([mixed[1].T, mixed[2]], axis=1)
    two = compress(jnp.concatenate([top, bottom], axis=0), keep, work)
    overall = jnp.concatenate([exact(two[:, :keep], one), exact(two[:, keep:], one)], axis=1)
    fh, fl = split(overall)
    both = jnp.concatenate([fh, fl], axis=0)

    def step(b, _):
        place = pl.ds(pl.multiple_of(b * WB, WB), WB)
        wide = mm(both, high_ref[:, place])
        out_ref[:, place] = wide[:keep] + wide[keep:] + mm(fh, low_ref[:, place])
        return 0

    lax.fori_loop(0, out_ref.shape[1] // WB, step, 0)


def body(source, band_values, offsets):
    devices = lax.axis_size("rows")
    rows, width = source.shape
    up = [(i, i + 1) for i in range(devices - 1)]
    down = [(i + 1, i) for i in range(devices - 1)]

    def extended(x, reach):
        low = lax.ppermute(x[:, width - reach :], "rows", up)
        high = lax.ppermute(x[:, :reach], "rows", down)
        return jnp.concatenate([low, x, high], axis=1)

    src = extended(source, 3 * HB)
    band = extended(band_values, 2 * HB)
    blocks = width // WB + 2
    wide = src.shape[1]
    high, low, gram = pl.pallas_call(
        functools.partial(powers_kernel, float(width * devices)),
        out_shape=[
            jax.ShapeDtypeStruct((4 * rows, width), jnp.bfloat16),
            jax.ShapeDtypeStruct((4 * rows, width), jnp.bfloat16),
            jax.ShapeDtypeStruct((2, 4 * rows, 2 * rows), jnp.float32),
        ],
        scratch_shapes=[
            pltpu.VMEM((3, rows, wide), jnp.bfloat16),
            pltpu.VMEM((3, rows, wide), jnp.bfloat16),
            pltpu.VMEM((blocks, WB, 2 * WB), jnp.bfloat16),
            pltpu.VMEM((blocks, WB, 2 * WB), jnp.bfloat16),
        ],
        compiler_params=pltpu.CompilerParams(vmem_limit_bytes=48 * 1024 * 1024),
        name="powers",
    )(src, band, offsets.reshape(-1, 1))

    parts = gram.reshape(devices, -1, 128)
    mine = lax.all_to_all(parts, "rows", 0, 0, tiled=True).sum(axis=0)
    copies = jnp.broadcast_to(mine, (devices, *mine.shape))
    gram = lax.all_to_all(copies, "rows", 0, 0, tiled=True).reshape(gram.shape)

    return pl.pallas_call(
        finish_kernel,
        out_shape=jax.ShapeDtypeStruct((2 * rows, width), jnp.float32),
        scratch_shapes=[pltpu.VMEM((2 * rows, 6 * rows), jnp.float32)],
        compiler_params=pltpu.CompilerParams(vmem_limit_bytes=48 * 1024 * 1024),
        name="finish",
    )(gram, high, low)


def solution(mesh):
    in_specs = (P(None, "rows"), P(None, "rows"), P())
    return jax.shard_map(
        body, mesh=mesh, in_specs=in_specs, out_specs=P(None, "rows"), check_vma=False
    )
```

time: 571 us -> 135 us (0.24); the launches traced: 565 us -> 135 us
  local copies, waits for them, and re-layouts: 293 us -> 5.84 us
  other arithmetic: 95.9 us -> 3.16 us
  Pallas kernels: 0 us -> 55.5 us
  matrix products: 52.3 us -> 0 us
  blocking collectives: 77.4 us -> 55.9 us
  starting transfers between devices: 27.9 us -> 12.4 us
  waiting for transfers between devices: 17.4 us -> 2.26 us
    unnamed x37 -> x6, local copies, waits for them, and re-layouts: 154 us -> 2.91 us
    gather x2 -> x0, local copies, waits for them, and re-layouts: 96.1 us -> none  [pack_upper(): return square[upper_rows, upper_cols]]
    another operation x20 -> x0, other arithmetic: 92 us -> none  [the longest x12 49.9 us: compress(): factor = jnp.linalg.cholesky(metric)]
    pallas_call x0 -> x2, Pallas kernels: none -> 55.5 us  [the longest x1 29.6 us: body(): pl.pallas_call(functools.partial(powers_kernel, float(width * devices)),...]
    dot_general x20 -> x0, matrix products: 51.1 us -> none  [the longest x3 30.7 us: apply_band(): jnp.einsum('cbj,brj->cbr', windows, blocked, precision=lax.Precision.HIGH...]
    all_to_all x4 -> x2, blocking collectives: 77.4 us -> 55.9 us  [the longest x1 34.6 us: body(): mine = lax.all_to_all(parts, 'rows', 0, 0, tiled=True).sum(axis=0)]
    scatter x3 -> x0, local copies, waits for them, and re-layouts: 17.4 us -> none  [the longest x1 17.2 us: band_blocks(): return blocked.at[:, row_index, columns].set(values)]
    all_to_all x2 -> x0, waiting for transfers between devices: 11 us -> none  [copy_for_each(): return lax.all_to_all(copies, axis, split_axis=0, concat_axis=0, tiled=True)]
  transfers between devices with their start and end apart: 8 -> 4, of which waited for: 4 -> 1; matrix products, arithmetic and copies ran while one was open for 14% -> 2% of each run, Pallas kernels for 0% -> 0%
where the time goes in v1:
time: 135 us
  blocking collectives  55.9 us (41%)
  Pallas kernels  55.5 us (41%)
  starting transfers between devices  12.4 us (9%)
  local copies, waits for them, and re-layouts  5.84 us (4%)
  other arithmetic  3.16 us (2%)
  waiting for transfers between devices  2.26 us (2%)
    all_to_all x1, blocking collectives, body(): mine = lax.all_to_all(parts, 'rows', 0, 0, tiled=True).sum(axis=0)  34.6 us
    pallas_call x1, Pallas kernels, body(): pl.pallas_call(functools.partial(powers_kernel, float(width * devices)),...  29.6 us
    pallas_call x1, Pallas kernels, body(): pl.pallas_call(finish_kernel, out_shape=jax.ShapeDtypeStruct((2 * rows, w...  25.8 us
    all_to_all x1, blocking collectives, body(): gram = lax.all_to_all(copies, 'rows', 0, 0, tiled=True).reshape(gram.shape)  21.2 us
    ppermute x2, starting transfers between devices, extended(): low = lax.ppermute(x[:, width - reach:], 'rows', up)  8.57 us
    ppermute x2, starting transfers between devices, extended(): high = lax.ppermute(x[:, :reach], 'rows', down)  3.84 us
    unnamed x6, local copies, waits for them, and re-layouts  2.91 us
    concatenate x2, other arithmetic, extended(): return jnp.concatenate([low, x, high], axis=1)  2.89 us
  transfers between devices with their start and end apart: 4, of which 1 were waited for; matrix products, arithmetic and copies ran while one was open for 2% of the time, Pallas kernels for 0%

profile of v1, /device:TPU:1, one launch (start us, length us, event | category | flops | bytes accessed | tf_op | source)
XLA Modules:
  0.0 135.1 jit_solution(1876502259765609576)
XLA Ops:
  0.0 0.0 copy-start.2
  0.0 1.1 fusion.1
  1.1 4.9 %collective-permute-start = (f32[64,384]{1,0:T(8,128)S(1)}, f32[64,384]{1,0:T(8,128)S(1)}, u32[]{:S(2)}, u32[]{:S(2)}) collective-permute-start(f32[64,384]{1,0:T(8,128)S(1)} %get-tuple-element.13), channel_id=1, source_target_pairs={{0,1},{1,2},{2,3},{3,4},{4,5},{5,6},{6,7},{7,8},{8,9},{9,10},{10,1... | collective-permute-start | bytes 294920 | tf_op jit(solution)/shard_map/ppermute | solution.py:190
  6.0 1.9 %collective-permute-start.1 = (f32[64,384]{1,0:T(8,128)S(1)}, f32[64,384]{1,0:T(8,128)S(1)}, u32[]{:S(2)}, u32[]{:S(2)}) collective-permute-start(f32[64,384]{1,0:T(8,128)S(1)} %get-tuple-element.14), channel_id=1, source_target_pairs={{1,0},{2,1},{3,2},{4,3},{5,4},{6,5},{7,6},{8,7},{9,8},{10,9},{11,1... | collective-permute-start | bytes 294920 | tf_op jit(solution)/shard_map/ppermute | solution.py:191
  8.0 1.0 fusion
  9.0 3.6 %collective-permute-start.2 = (f32[128,256]{1,0:T(8,128)S(1)}, f32[128,256]{1,0:T(8,128)S(1)}, u32[]{:S(2)}, u32[]{:S(2)}) collective-permute-start(f32[128,256]{1,0:T(8,128)S(1)} %get-tuple-element.11), channel_id=1, source_target_pairs={{0,1},{1,2},{2,3},{3,4},{4,5},{5,6},{6,7},{7,8},{8,9},{9,10},{10,1... | collective-permute-start | bytes 393224 | tf_op jit(solution)/shard_map/ppermute | solution.py:190
  12.6 1.9 %collective-permute-start.3 = (f32[128,256]{1,0:T(8,128)S(1)}, f32[128,256]{1,0:T(8,128)S(1)}, u32[]{:S(2)}, u32[]{:S(2)}) collective-permute-start(f32[128,256]{1,0:T(8,128)S(1)} %get-tuple-element.12), channel_id=1, source_target_pairs={{1,0},{2,1},{3,2},{4,3},{5,4},{6,5},{7,6},{8,7},{9,8},{10,9},{11,1... | collective-permute-start | bytes 393224 | tf_op jit(solution)/shard_map/ppermute | solution.py:191
  14.5 0.8 copy.4.off_ref
  15.3 0.0 collective-permute-done
  15.3 0.0 collective-permute-done.1
  15.3 1.3 pad_maximum_fusion.1.src_ref
  16.6 0.0 collective-permute-done.2
  16.6 2.3 %collective-permute-done.3 = f32[128,256]{1,0:T(8,128)S(1)} collective-permute-done((f32[128,256]{1,0:T(8,128)S(1)}, f32[128,256]{1,0:T(8,128)S(1)}, u32[]{:S(2)}, u32[]{:S(2)}) %collective-permute-start.3) | collective-permute-done | bytes 131104 | tf_op jit(solution)/shard_map/ppermute | solution.py:191
  18.9 0.0 copy-done.2
  18.9 1.6 %pad_maximum_fusion.band_ref = f32[128,4608]{1,0:T(8,128)} fusion(f32[128,256]{1,0:T(8,128)S(1)} %collective-permute-done.3, f32[128,4096]{1,0:T(8,128)S(1)} %copy-done.2, f32[128,256]{1,0:T(8,128)S(1)} %collective-permute-done.2), kind=kLoop, calls=%fused_computation | loop fusion | flops 1179648 | bytes 4718592 | tf_op jit(solution)/shard_map/concatenate | solution.py:192
  20.5 29.6 %powers.1 = (bf16[256,4096]{1,0:T(8,128)(2,1)S(1)}, bf16[256,4096]{1,0:T(8,128)(2,1)S(1)}, f32[2,256,128]{2,1,0:T(8,128)S(1)}) custom-call(f32[64,4864]{1,0:T(8,128)S(1)} %pad_maximum_fusion.1.src_ref, f32[128,4608]{1,0:T(8,128)} %pad_maximum_fusion.band_ref, s32[128,1]{1,0:T(8,128)S(1)} %copy.4.off_ref), custom_call_target="tpu_custom_call" | custom-call | tf_op jit(solution)/shard_map/powers/pallas_call | solution.py:198
  50.1 0.0 copy-start
  50.1 1.3 copy-done
  51.4 34.6 %all_to_all.10 = f32[256,2,128]{2,1,0:T(2,128)S(1)} all-to-all(f32[256,2,128]{2,1,0:T(2,128)S(1)} %bitcast.4), channel_id=1, replica_groups=mesh['rows'=256] {'rows'}, dimensions={0} | all-to-all | bytes 524288 | tf_op jit(solution)/shard_map/all_to_all | solution.py:216
  86.0 0.3 reduce_sum.9
  86.3 0.1 broadcast_in_dim.3
  86.4 21.2 %all_to_all.11 = f32[256,2,128]{2,1,0:T(2,128)S(1)} all-to-all(f32[256,2,128]{2,1,0:T(2,128)S(1)} %broadcast_in_dim.3), channel_id=1, replica_groups=mesh['rows'=256] {'rows'}, dimensions={0} | all-to-all | bytes 524288 | tf_op jit(solution)/shard_map/all_to_all | solution.py:218
  107.6 1.6 %copy-done.1 = bf16[256,4096]{1,0:T(8,128)(2,1)S(1)} copy-done((bf16[256,4096]{1,0:T(8,128)(2,1)S(1)}, bf16[256,4096]{1,0:T(8,128)(2,1)}, u32[]{:S(2)}) %copy-start.1) | copy-done | bytes 2097176
  109.2 25.8 %finish.1 = f32[128,4096]{1,0:T(8,128)} custom-call(f32[2,256,128]{2,1,0:T(8,128)S(1)} %bitcast.3, bf16[256,4096]{1,0:T(8,128)(2,1)S(1)} %get-tuple-element.9.high_ref, bf16[256,4096]{1,0:T(8,128)(2,1)S(1)} %copy-done.1), custom_call_target="tpu_custom_call" | custom-call | tf_op jit(solution)/shard_map/finish/pallas_call | solution.py:220
  (1 shorter events, 0.0 us)
Async XLA Ops:
  0.0 18.9 %copy-start.2 = (f32[128,4096]{1,0:T(8,128)S(1)}, f32[128,4096]{1,0:T(8,128)}, u32[]{:S(2)}) copy-start(f32[128,4096]{1,0:T(8,128)} %param.4) | copy-start | bytes 6291460
  1.1 14.2 %collective-permute-start = (f32[64,384]{1,0:T(8,128)S(1)}, f32[64,384]{1,0:T(8,128)S(1)}, u32[]{:S(2)}, u32[]{:S(2)}) collective-permute-start(f32[64,384]{1,0:T(8,128)S(1)} %get-tuple-element.13), channel_id=1, source_target_pairs={{0,1},{1,2},{2,3},{3,4},{4,5},{5,6},{6,7},{7,8},{8,9},{9,10},{10,1... | collective-permute-start | bytes 294920 | tf_op jit(solution)/shard_map/ppermute | solution.py:190
  6.0 9.3 %collective-permute-start.1 = (f32[64,384]{1,0:T(8,128)S(1)}, f32[64,384]{1,0:T(8,128)S(1)}, u32[]{:S(2)}, u32[]{:S(2)}) collective-permute-start(f32[64,384]{1,0:T(8,128)S(1)} %get-tuple-element.14), channel_id=1, source_target_pairs={{1,0},{2,1},{3,2},{4,3},{5,4},{6,5},{7,6},{8,7},{9,8},{10,9},{11,1... | collective-permute-start | bytes 294920 | tf_op jit(solution)/shard_map/ppermute | solution.py:191
  9.0 7.7 %collective-permute-start.2 = (f32[128,256]{1,0:T(8,128)S(1)}, f32[128,256]{1,0:T(8,128)S(1)}, u32[]{:S(2)}, u32[]{:S(2)}) collective-permute-start(f32[128,256]{1,0:T(8,128)S(1)} %get-tuple-element.11), channel_id=1, source_target_pairs={{0,1},{1,2},{2,3},{3,4},{4,5},{5,6},{6,7},{7,8},{8,9},{9,10},{10,1... | collective-permute-start | bytes 393224 | tf_op jit(solution)/shard_map/ppermute | solution.py:190
  12.6 6.3 %collective-permute-start.3 = (f32[128,256]{1,0:T(8,128)S(1)}, f32[128,256]{1,0:T(8,128)S(1)}, u32[]{:S(2)}, u32[]{:S(2)}) collective-permute-start(f32[128,256]{1,0:T(8,128)S(1)} %get-tuple-element.12), channel_id=1, source_target_pairs={{1,0},{2,1},{3,2},{4,3},{5,4},{6,5},{7,6},{8,7},{9,8},{10,9},{11,1... | collective-permute-start | bytes 393224 | tf_op jit(solution)/shard_map/ppermute | solution.py:191
  50.1 1.3 copy-start
  107.6 1.6 %copy-start.1 = (bf16[256,4096]{1,0:T(8,128)(2,1)S(1)}, bf16[256,4096]{1,0:T(8,128)(2,1)}, u32[]{:S(2)}) copy-start(bf16[256,4096]{1,0:T(8,128)(2,1)} %copy-done) | copy-start | bytes 6291460

commit v2 on v1

v2 whole, which is shorter than its diff:
```python
import functools

import jax
import jax.numpy as jnp
from jax import lax
from jax.experimental import pallas as pl
from jax.experimental.pallas import tpu as pltpu
from jax.sharding import Mesh
from jax.sharding import PartitionSpec as P

HB = 128
WB = 256
SPAN = 2 * WB
ROWS = ("far", "near")
NN = (((1,), (0,)), ((), ()))
NT = (((1,), (1,)), ((), ()))


def split(x):
    high = x.astype(jnp.bfloat16)
    return high, (x - high.astype(jnp.float32)).astype(jnp.bfloat16)


def mm(a, b, dims=NN):
    return lax.dot_general(a, b, dims, preferred_element_type=jnp.float32)


def exact(a, b, dims=NN):
    return lax.dot_general(
        a, b, dims, precision=lax.Precision.HIGHEST, preferred_element_type=jnp.float32
    )


def picker(off_ref):
    lanes = lax.broadcasted_iota(jnp.int32, (off_ref.shape[0], SPAN), 1)
    pick = jnp.where(lanes == off_ref[...] + HB, 1.0, 0.0).astype(jnp.bfloat16)
    return jnp.concatenate([pick, pick], axis=0)


def band_block(values, pick):
    diag = mm(jnp.concatenate(split(values.T), axis=1), pick)
    return split(pltpu.roll(diag, 0, 1, stride=1, stride_axis=0).T)


def blocks_kernel(band_ref, off_ref, wh, wl, pick_ref):
    pick_ref[...] = picker(off_ref)

    def build(b, _):
        at = pl.multiple_of(b * WB, WB)
        wh[b], wl[b] = band_block(band_ref[:, pl.ds(at, WB)], pick_ref[...])
        return 0

    lax.fori_loop(0, wh.shape[0], build, 0, unroll=2)


def powers_kernel(
    total, src_ref, low_in, high_in, off_ref, wh, wl, high_ref, low_ref, gram_ref, xs, eh, el
):
    rows, width = src_ref.shape
    inner = width // WB
    reach = 3 * HB
    edges = [(low_in, 0, 0), (high_in, 1, reach + width)]
    pick = picker(off_ref)
    for ref, side, at in edges:
        high, low = split(ref[:, :reach])
        xs[0, :rows, at : at + reach] = high
        xs[0, rows:, at : at + reach] = low
        values = jnp.concatenate([ref[:, reach : reach + WB], ref[:, reach + WB :]], axis=0)
        eh[side], el[side] = band_block(values, pick)

    def place(b, _):
        at = pl.multiple_of(b * WB, WB)
        high, low = split(src_ref[:, pl.ds(at, WB)])
        high_ref[:rows, pl.ds(at, WB)] = high
        low_ref[:rows, pl.ds(at, WB)] = low
        into = pl.ds(pl.multiple_of(b * WB + reach, HB), WB)
        xs[0, :rows, into] = high
        xs[0, rows:, into] = low
        return 0

    lax.fori_loop(0, inner, place, 0, unroll=2)
    for power in (1, 2):
        for at in (0, xs.shape[2] - HB):
            xs[power, :, at : at + HB] = jnp.zeros((2 * rows, HB), jnp.bfloat16)

    def apply(power, at, by_high, by_low):
        window = xs[power - 1, :, pl.ds(at, SPAN)]
        both = mm(window, by_high)
        return split(both[:rows] + both[rows:] + mm(window[:rows], by_low))

    def keep(power, at, pair):
        for part in range(2):
            xs[power, part * rows : (part + 1) * rows, pl.ds(at, WB)] = pair[part]

    for power in (1, 2, 3):
        if power < 3:
            for _, side, at in edges:
                at = at if side == 0 else at - HB
                keep(power, at + HB, apply(power, at, eh[side], el[side]))

        def step(b, _):
            at = pl.multiple_of(b * WB, WB)
            pair = apply(power, pl.multiple_of(at + WB, WB), wh[b], wl[b])
            high_ref[power * rows : (power + 1) * rows, pl.ds(at, WB)] = pair[0]
            low_ref[power * rows : (power + 1) * rows, pl.ds(at, WB)] = pair[1]
            if power < 3:
                keep(power, pl.multiple_of(at + reach, HB), pair)
            return 0

        lax.fori_loop(0, inner, step, 0, unroll=4)

    tall = high_ref[...]
    gram = mm(tall, tall, NT) + 2.0 * mm(tall, low_ref[...], NT)
    pack(gram_ref, (gram + gram.T) * (0.5 / total))


def places(order):
    shape = (order, order)
    down = lax.broadcasted_iota(jnp.int32, shape, 0)
    return lax.broadcasted_iota(jnp.int32, shape, 1) - down


def pack(ref, gram):
    half = ref.shape[2]
    part = half // ref.shape[0]
    across = places(half)
    tail = gram[half:, half:]
    ref[:, :part] = gram[:half, half:].reshape(-1, part, half)
    both = jnp.where(across >= 0, gram[:half, :half], tail)
    ref[:, part : 2 * part] = both.reshape(-1, part, half)
    ref[:, 2 * part :] = jnp.zeros((ref.shape[0], 8, half), jnp.float32)
    middle = jnp.sum(jnp.where(across == 0, tail, 0.0), axis=0, keepdims=True)
    ref[0, 2 * part : 2 * part + 1] = middle


def unpack(ref):
    half = ref.shape[2]
    part = half // ref.shape[0]
    across = places(half)
    cross = ref[:, :part].reshape(half, half)
    both = ref[:, part : 2 * part].reshape(half, half)
    middle = jnp.broadcast_to(ref[0, 2 * part : 2 * part + 1], (half, half))
    upper = jnp.where(across > 0, both, 0.0)
    lower = jnp.where(across < 0, both, 0.0)
    head = upper + upper.T + jnp.where(across == 0, both, 0.0)
    tail = lower + lower.T + jnp.where(across == 0, middle, 0.0)
    return head, cross, tail


def lane_copy(x, lane):
    return jnp.broadcast_to(x[:, lane : lane + 1], (8, 128))


def row_copy(x, row):
    return jnp.broadcast_to(x[row : row + 1, :], (8, 128))


def eliminate(work, tiles):
    order = work.shape[0]
    sub = lax.broadcasted_iota(jnp.int32, (8, 128), 0)

    def tile(g, t):
        return slice(8 * g, 8 * g + 8), slice(128 * t, 128 * t + 128)

    for kb in range(order // 8):
        own = [work[tile(kb, t)] for t in range(tiles)]
        cols = [lane_copy(own[0], 8 * kb + j) for j in range(8)]
        inverses, cross, tops = [], [], []
        pivots = jnp.ones((8, 128), jnp.float32)
        for k in range(8):
            pivot = row_copy(cols[k], k)
            inverse = 1.0 / pivot
            pivots = jnp.where(sub == k, pivot, pivots)
            m = jnp.where(sub > k, cols[k] * inverse, 0.0)
            crossing = [row_copy(cols[j], k) for j in range(k + 1, 8)]
            top = [row_copy(x, k) for x in own]
            for j in range(k + 1, 8):
                cols[j] = cols[j] - m * crossing[j - k - 1]
            own = [x - m * y for x, y in zip(own, top)]
            inverses.append(inverse)
            cross.append(crossing)
            tops.append(top)
        scale = lax.rsqrt(pivots)
        for t in range(1, tiles):
            work[tile(kb, t)] = own[t] * scale
        for g in range(kb + 1, order // 8):
            rest = [work[tile(g, t)] for t in range(tiles)]
            q = [lane_copy(rest[0], 8 * kb + j) for j in range(8)]
            for k in range(8):
                m = q[k] * inverses[k]
                for j in range(k + 1, 8):
                    q[j] = q[j] - m * cross[k][j - k - 1]
                rest = [x - m * y for x, y in zip(rest, tops[k])]
            for t in range(tiles):
                work[tile(g, t)] = rest[t]


def compress(gram, retain, work):
    order = gram.shape[0]
    spanning = gram[:retain]
    for turn in range(2):
        if turn > 0:
            spanning = exact(work[:, retain : retain + order], gram)
        mapped = exact(spanning, gram)
        metric = exact(mapped, spanning, NT)
        work[:, :retain] = 0.5 * (metric + metric.T)
        work[:, retain : retain + order] = spanning
        eliminate(work, (retain + order) // 128)
    return work[:, retain : retain + order]


def finish_kernel(gram_ref, high_ref, low_ref, out_ref, work):
    keep = out_ref.shape[0]
    g11, g12, g22 = unpack(gram_ref)
    one = compress(g11, keep, work)
    mixed = [exact(exact(one, g), one, NT) for g in (g11, g12, g22)]
    top = jnp.concatenate([mixed[0], mixed[1]], axis=1)
    bottom = jnp.concatenate([mixed[1].T, mixed[2]], axis=1)
    two = compress(jnp.concatenate([top, bottom], axis=0), keep, work)
    overall = jnp.concatenate([exact(two[:, :keep], one), exact(two[:, keep:], one)], axis=1)
    fh, fl = split(overall)
    both = jnp.concatenate([fh, fl], axis=0)

    def step(b, _):
        place = pl.ds(pl.multiple_of(b * WB, WB), WB)
        wide = mm(both, high_ref[:, place])
        out_ref[:, place] = wide[:keep] + wide[keep:] + mm(fh, low_ref[:, place])
        return 0

    lax.fori_loop(0, out_ref.shape[1] // WB, step, 0)


def exchange(blocks, axis):
    return lax.all_to_all(blocks, axis, 0, 0, tiled=True)


def copies(x, axis):
    return exchange(jnp.broadcast_to(x, (lax.axis_size(axis), *x.shape)), axis)


def body(source, band_values, offsets):
    devices = lax.axis_size(ROWS)
    group = lax.axis_size("near")
    rows, width = source.shape
    reach = 3 * HB
    inner = width // WB
    up = [(i, i + 1) for i in range(devices - 1)]
    down = [(i + 1, i) for i in range(devices - 1)]

    def packed(far, near):
        return jnp.concatenate([far, near[:rows], near[rows:]], axis=1)

    low = lax.ppermute(packed(source[:, width - reach :], band_values[:, width - WB :]), ROWS, up)
    high = lax.ppermute(packed(source[:, :reach], band_values[:, :WB]), ROWS, down)
    offsets = offsets.reshape(-1, 1)
    blocks = jax.ShapeDtypeStruct((inner, SPAN, WB), jnp.bfloat16)
    by_high, by_low = pl.pallas_call(
        blocks_kernel,
        out_shape=[blocks, blocks],
        scratch_shapes=[pltpu.VMEM((2 * HB, SPAN), jnp.bfloat16)],
        compiler_params=pltpu.CompilerParams(vmem_limit_bytes=12 * 1024 * 1024),
        cost_estimate=pl.CostEstimate(
            flops=10_000_000_000, bytes_accessed=12_000_000, transcendentals=0
        ),
        name="blocks",
    )(band_values, offsets)
    wide = width + 2 * reach
    high, low, gram = pl.pallas_call(
        functools.partial(powers_kernel, float(width * devices)),
        out_shape=[
            jax.ShapeDtypeStruct((4 * rows, width), jnp.bfloat16),
            jax.ShapeDtypeStruct((4 * rows, width), jnp.bfloat16),
            jax.ShapeDtypeStruct((group, 4 * rows // group + 8, 2 * rows), jnp.float32),
        ],
        scratch_shapes=[
            pltpu.VMEM((3, 2 * rows, wide), jnp.bfloat16),
            pltpu.VMEM((2, SPAN, WB), jnp.bfloat16),
            pltpu.VMEM((2, SPAN, WB), jnp.bfloat16),
        ],
        compiler_params=pltpu.CompilerParams(vmem_limit_bytes=16 * 1024 * 1024),
        name="powers",
    )(source, low, high, offsets, by_high, by_low)

    gram = exchange(gram, "near").sum(axis=0)
    gram = copies(gram, "far").sum(axis=0)
    gram = copies(gram, "near")

    return pl.pallas_call(
        finish_kernel,
        out_shape=jax.ShapeDtypeStruct((2 * rows, width), jnp.float32),
        scratch_shapes=[pltpu.VMEM((2 * rows, 6 * rows), jnp.float32)],
        compiler_params=pltpu.CompilerParams(vmem_limit_bytes=16 * 1024 * 1024),
        name="finish",
    )(gram, high, low)


def solution(mesh):
    devices = mesh.devices.size
    near = 1 << (devices.bit_length() // 2)
    grid = Mesh(mesh.devices.reshape(devices // near, near), ROWS)
    split_rows = P(None, ROWS)
    return jax.shard_map(
        body,
        mesh=grid,
        in_specs=(split_rows, split_rows, P()),
        out_specs=split_rows,
        check_vma=False,
    )
```

time: 135 us -> 110 us (0.81)
  blocking collectives: 55.9 us -> 47.7 us
  Pallas kernels: 55.5 us -> 47.7 us
  starting transfers between devices: 12.4 us -> 6.84 us
  other arithmetic: 3.16 us -> 0.08 us
  waiting for transfers between devices: 2.26 us -> 0.01 us
  local copies, waits for them, and re-layouts: 5.84 us -> 7.2 us
    pallas_call x1, Pallas kernels: 29.6 us -> 13.1 us  [body(): pl.pallas_call(functools.partial(powers_kernel, float(width * devices)),...]
    pallas_call x0 -> x1, Pallas kernels: none -> 8.71 us  [body(): pl.pallas_call(blocks_kernel, out_shape=[blocks, blocks], scratch_shapes=...]
    all_to_all x2 -> x3, blocking collectives: 55.9 us -> 47.7 us  [exchange(): return lax.all_to_all(blocks, axis, 0, 0, tiled=True)]
    ppermute x4 -> x2, starting transfers between devices: 12.4 us -> 6.84 us  [the longest x1 4.92 us: body(): lax.ppermute(packed(source[:, width - reach:], band_values[:, width - WB:...]
    concatenate x2, other arithmetic: 2.89 us -> 0.03 us  [packed(): return jnp.concatenate([far, near[:rows], near[rows:]], axis=1)]
    ppermute x4 -> x2, waiting for transfers between devices: 2.26 us -> 0.01 us  [the longest x1 0.01 us: body(): lax.ppermute(packed(source[:, width - reach:], band_values[:, width - WB:...]
    unnamed x6 -> x8, local copies, waits for them, and re-layouts: 2.91 us -> 4.49 us
  transfers between devices with their start and end apart: 4 -> 2, of which waited for: 1 -> 0; matrix products, arithmetic and copies ran while one was open for 2% -> 1% of each run, Pallas kernels for 0% -> 8%
where the time goes in v2:
time: 110 us
  Pallas kernels  47.7 us (43%)
  blocking collectives  47.7 us (43%)
  local copies, waits for them, and re-layouts  7.2 us (7%)
  starting transfers between devices  6.84 us (6%)
    all_to_all x3, blocking collectives, exchange(): return lax.all_to_all(blocks, axis, 0, 0, tiled=True)  47.7 us
    pallas_call x1, Pallas kernels, body(): pl.pallas_call(finish_kernel, out_shape=jax.ShapeDtypeStruct((2 * rows, w...  25.9 us
    pallas_call x1, Pallas kernels, body(): pl.pallas_call(functools.partial(powers_kernel, float(width * devices)),...  13.1 us
    pallas_call x1, Pallas kernels, body(): pl.pallas_call(blocks_kernel, out_shape=[blocks, blocks], scratch_shapes=...  8.71 us
    ppermute x1, starting transfers between devices, body(): lax.ppermute(packed(source[:, width - reach:], band_values[:, width - WB:...  4.92 us
    unnamed x8, local copies, waits for them, and re-layouts  4.49 us
  transfers between devices with their start and end apart: 2, of which 0 were waited for; matrix products, arithmetic and copies ran while one was open for 1% of the time, Pallas kernels for 8%

profile of v2, /device:TPU:1, one launch (start us, length us, event | category | flops | bytes accessed | tf_op | source)
XLA Modules:
  0.0 109.7 jit_solution(9453442444175487464)
XLA Ops:
  0.0 1.0 fusion.1
  1.0 1.0 fusion
  1.9 4.9 %collective-permute-start = (f32[64,896]{1,0:T(8,128)S(1)}, f32[64,896]{1,0:T(8,128)S(1)}, u32[]{:S(2)}, u32[]{:S(2)}) collective-permute-start(f32[64,896]{1,0:T(8,128)S(1)} %pad_maximum_fusion), channel_id=1, source_target_pairs={{0,1},{1,2},{2,3},{3,4},{4,5},{5,6},{6,7},{7,8},{8,9},{9,10},{10,1... | collective-permute-start | bytes 688136 | tf_op jit(solution)/shard_map/ppermute | solution.py:253
  6.9 1.9 %collective-permute-start.1 = (f32[64,896]{1,0:T(8,128)S(1)}, f32[64,896]{1,0:T(8,128)S(1)}, u32[]{:S(2)}, u32[]{:S(2)}) collective-permute-start(f32[64,896]{1,0:T(8,128)S(1)} %pad_maximum_fusion.1), channel_id=1, source_target_pairs={{1,0},{2,1},{3,2},{4,3},{5,4},{6,5},{7,6},{8,7},{9,8},{10,9},{11,1... | collective-permute-start | bytes 688136 | tf_op jit(solution)/shard_map/ppermute | solution.py:254
  8.8 0.8 copy.7.off_ref
  9.6 0.0 copy-start.3
  9.6 1.6 %copy-done.3 = f32[128,4096]{1,0:T(8,128)S(1)} copy-done((f32[128,4096]{1,0:T(8,128)S(1)}, f32[128,4096]{1,0:T(8,128)}, u32[]{:S(2)}) %copy-start.3) | copy-done | bytes 2097176
  11.2 0.0 copy-start.2
  11.2 8.7 %blocks.1 = (bf16[16,512,256]{2,1,0:T(8,128)(2,1)S(1)}, bf16[16,512,256]{2,1,0:T(8,128)(2,1)S(1)}) custom-call(f32[128,4096]{1,0:T(8,128)S(1)} %copy-done.3, s32[128,1]{1,0:T(8,128)S(1)} %copy.7.off_ref), custom_call_target="tpu_custom_call" | custom-call | flops 10000000000 | bytes 12000000 | tf_op jit(solution)/shard_map/blocks/pallas_call | solution.py:257
  19.9 0.0 collective-permute-done.low_in
  19.9 0.0 collective-permute-done.1.high_in
  19.9 0.0 copy-done.2
  19.9 13.1 %powers.1 = (bf16[256,4096]{1,0:T(8,128)(2,1)S(1)}, bf16[256,4096]{1,0:T(8,128)(2,1)S(1)}, f32[16,24,128]{2,1,0:T(8,128)S(1)}) custom-call(f32[64,4096]{1,0:T(8,128)S(1)} %copy-done.2, f32[64,896]{1,0:T(8,128)S(1)} %collective-permute-done.low_in, f32[64,896]{1,0:T(8,128)S(1)} %collective-permute-done.1.high_in, s32[128,1]{1,0:T(8,128)S(1)} %copy.7.off_ref, ...), custom_call_target="tpu_custom_call" | custom-call | tf_op jit(solution)/shard_map/powers/pallas_call | solution.py:268
  33.1 0.0 copy-start
  33.1 1.3 %copy-done = bf16[256,4096]{1,0:T(8,128)(2,1)} copy-done((bf16[256,4096]{1,0:T(8,128)(2,1)}, bf16[256,4096]{1,0:T(8,128)(2,1)S(1)}, u32[]{:S(2)}) %copy-start) | copy-done | bytes 2097176
  34.4 19.9 %all_to_all.15 = f32[16,24,128]{2,1,0:T(8,128)S(1)} all-to-all(f32[16,24,128]{2,1,0:T(8,128)S(1)} %get-tuple-element.12), channel_id=1, replica_groups=mesh['far'=16,'near'=16] {'near'}, dimensions={0} | all-to-all | bytes 393216 | tf_op jit(solution)/shard_map/all_to_all | solution.py:234
  54.3 14.5 %all_to_all.16 = f32[16,24,128]{2,1,0:T(8,128)S(1)} all-to-all(f32[16,24,128]{2,1,0:T(8,128)S(1)} %broadcast_in_dim.6), channel_id=1, replica_groups=mesh['far'=16,'near'=16] {'far'}, dimensions={0} | all-to-all | bytes 393216 | tf_op jit(solution)/shard_map/all_to_all | solution.py:234
  68.9 13.3 %all_to_all.17.gram_ref = f32[16,24,128]{2,1,0:T(8,128)S(1)} all-to-all(f32[16,24,128]{2,1,0:T(8,128)S(1)} %broadcast_in_dim.7), channel_id=1, replica_groups=mesh['far'=16,'near'=16] {'near'}, dimensions={0} | all-to-all | bytes 393216 | tf_op jit(solution)/shard_map/all_to_all | solution.py:234
  82.2 0.0 copy-start.1
  82.2 1.6 %copy-done.1 = bf16[256,4096]{1,0:T(8,128)(2,1)S(1)} copy-done((bf16[256,4096]{1,0:T(8,128)(2,1)S(1)}, bf16[256,4096]{1,0:T(8,128)(2,1)}, u32[]{:S(2)}) %copy-start.1) | copy-done | bytes 2097176
  83.8 25.9 %finish.1 = f32[128,4096]{1,0:T(8,128)} custom-call(f32[16,24,128]{2,1,0:T(8,128)S(1)} %all_to_all.17.gram_ref, bf16[256,4096]{1,0:T(8,128)(2,1)S(1)} %get-tuple-element.13.high_ref, bf16[256,4096]{1,0:T(8,128)(2,1)S(1)} %copy-done.1), custom_call_target="tpu_custom_call" | custom-call | tf_op jit(solution)/shard_map/finish/pallas_call | solution.py:288
  (6 shorter events, 0.1 us)
Async XLA Ops:
  1.9 18.0 %collective-permute-start = (f32[64,896]{1,0:T(8,128)S(1)}, f32[64,896]{1,0:T(8,128)S(1)}, u32[]{:S(2)}, u32[]{:S(2)}) collective-permute-start(f32[64,896]{1,0:T(8,128)S(1)} %pad_maximum_fusion), channel_id=1, source_target_pairs={{0,1},{1,2},{2,3},{3,4},{4,5},{5,6},{6,7},{7,8},{8,9},{9,10},{10,1... | collective-permute-start | bytes 688136 | tf_op jit(solution)/shard_map/ppermute | solution.py:253
  6.9 13.0 %collective-permute-start.1 = (f32[64,896]{1,0:T(8,128)S(1)}, f32[64,896]{1,0:T(8,128)S(1)}, u32[]{:S(2)}, u32[]{:S(2)}) collective-permute-start(f32[64,896]{1,0:T(8,128)S(1)} %pad_maximum_fusion.1), channel_id=1, source_target_pairs={{1,0},{2,1},{3,2},{4,3},{5,4},{6,5},{7,6},{8,7},{9,8},{10,9},{11,1... | collective-permute-start | bytes 688136 | tf_op jit(solution)/shard_map/ppermute | solution.py:254
  9.6 1.6 %copy-start.3 = (f32[128,4096]{1,0:T(8,128)S(1)}, f32[128,4096]{1,0:T(8,128)}, u32[]{:S(2)}) copy-start(f32[128,4096]{1,0:T(8,128)} %band_ref.1) | copy-start | bytes 6291460
  11.2 8.7 %copy-start.2 = (f32[64,4096]{1,0:T(8,128)S(1)}, f32[64,4096]{1,0:T(8,128)}, u32[]{:S(2)}) copy-start(f32[64,4096]{1,0:T(8,128)} %src_ref.1) | copy-start | bytes 3145732
  33.1 1.3 %copy-start = (bf16[256,4096]{1,0:T(8,128)(2,1)}, bf16[256,4096]{1,0:T(8,128)(2,1)S(1)}, u32[]{:S(2)}) copy-start(bf16[256,4096]{1,0:T(8,128)(2,1)S(1)} %get-tuple-element.14.low_ref) | copy-start | bytes 6291460
  82.2 1.6 %copy-start.1 = (bf16[256,4096]{1,0:T(8,128)(2,1)S(1)}, bf16[256,4096]{1,0:T(8,128)(2,1)}, u32[]{:S(2)}) copy-start(bf16[256,4096]{1,0:T(8,128)(2,1)} %copy-done) | copy-start | bytes 6291460

commit v3 on v2

--- a/solution.py
+++ b/solution.py
@@ -32,25 +32,34 @@
 
 
 def picker(off_ref):
-    lanes = lax.broadcasted_iota(jnp.int32, (off_ref.shape[0], SPAN), 1)
+    lanes = lax.broadcasted_iota(jnp.int32, (off_ref.shape[0], 3 * HB), 1)
     pick = jnp.where(lanes == off_ref[...] + HB, 1.0, 0.0).astype(jnp.bfloat16)
     return jnp.concatenate([pick, pick], axis=0)
 
 
-def band_block(values, pick):
-    diag = mm(jnp.concatenate(split(values.T), axis=1), pick)
-    return split(pltpu.roll(diag, 0, 1, stride=1, stride_axis=0).T)
-
-
-def blocks_kernel(band_ref, off_ref, wh, wl, pick_ref):
-    pick_ref[...] = picker(off_ref)
-
-    def build(b, _):
-        at = pl.multiple_of(b * WB, WB)
-        wh[b], wl[b] = band_block(band_ref[:, pl.ds(at, WB)], pick_ref[...])
-        return 0
-
-    lax.fori_loop(0, wh.shape[0], build, 0, unroll=2)
+def diagonals(values, pick):
+    return mm(jnp.concatenate(split(values.T), axis=1), pick)
+
+
+def place_block(diag, wh, wl, b):
+    for half in range(2):
+        rows = slice(half * HB, half * HB + HB)
+        band = pltpu.roll(diag[rows], 0, 1, stride=1, stride_axis=0)
+        high, low = split(band.T)
+        for ref, part in ((wh, high), (wl, low)):
+            ref[b, half * HB : half * HB + 3 * HB, rows] = part
+            empty = 3 * HB * (1 - half)
+            ref[b, empty : empty + HB, rows] = jnp.zeros((HB, HB), jnp.bfloat16)
+
+
+def blocks_kernel(band_ref, off_ref, wh, wl, diag_ref):
+    pick = picker(off_ref)
+    count = wh.shape[0]
+    for b in range(count + 1):
+        if b < count:
+            diag_ref[b % 2] = diagonals(band_ref[:, b * WB : b * WB + WB], pick)
+        if b > 0:
+            place_block(diag_ref[(b - 1) % 2], wh, wl, b - 1)
 
 
 def powers_kernel(
@@ -60,54 +69,45 @@
     inner = width // WB
     reach = 3 * HB
     edges = [(low_in, 0, 0), (high_in, 1, reach + width)]
+    for b in range(inner):
+        at = slice(b * WB, b * WB + WB)
+        into = slice(b * WB + reach, b * WB + reach + WB)
+        high, low = split(src_ref[:, at])
+        high_ref[:rows, at] = high
+        low_ref[:rows, at] = low
+        xs[0, :rows, into] = high
+        xs[0, rows:, into] = low
     pick = picker(off_ref)
     for ref, side, at in edges:
         high, low = split(ref[:, :reach])
         xs[0, :rows, at : at + reach] = high
         xs[0, rows:, at : at + reach] = low
         values = jnp.concatenate([ref[:, reach : reach + WB], ref[:, reach + WB :]], axis=0)
-        eh[side], el[side] = band_block(values, pick)
-
-    def place(b, _):
-        at = pl.multiple_of(b * WB, WB)
-        high, low = split(src_ref[:, pl.ds(at, WB)])
-        high_ref[:rows, pl.ds(at, WB)] = high
-        low_ref[:rows, pl.ds(at, WB)] = low
-        into = pl.ds(pl.multiple_of(b * WB + reach, HB), WB)
-        xs[0, :rows, into] = high
-        xs[0, rows:, into] = low
-        return 0
-
-    lax.fori_loop(0, inner, place, 0, unroll=2)
+        place_block(diagonals(values, pick), eh, el, side)
     for power in (1, 2):
         for at in (0, xs.shape[2] - HB):
             xs[power, :, at : at + HB] = jnp.zeros((2 * rows, HB), jnp.bfloat16)
 
     def apply(power, at, by_high, by_low):
-        window = xs[power - 1, :, pl.ds(at, SPAN)]
+        window = xs[power - 1, :, at : at + SPAN]
         both = mm(window, by_high)
         return split(both[:rows] + both[rows:] + mm(window[:rows], by_low))
 
-    def keep(power, at, pair):
-        for part in range(2):
-            xs[power, part * rows : (part + 1) * rows, pl.ds(at, WB)] = pair[part]
-
     for power in (1, 2, 3):
-        if power < 3:
-            for _, side, at in edges:
-                at = at if side == 0 else at - HB
-                keep(power, at + HB, apply(power, at, eh[side], el[side]))
-
-        def step(b, _):
-            at = pl.multiple_of(b * WB, WB)
-            pair = apply(power, pl.multiple_of(at + WB, WB), wh[b], wl[b])
-            high_ref[power * rows : (power + 1) * rows, pl.ds(at, WB)] = pair[0]
-            low_ref[power * rows : (power + 1) * rows, pl.ds(at, WB)] = pair[1]
+        inside = list(range(2, inner)) + [1, inner]
+        for b in inside + [0, inner + 1] * (power < 3):
+            if b in (0, inner + 1):
+                by = (eh[int(b > 0)], el[int(b > 0)])
+            else:
+                by = (wh[b - 1], wl[b - 1])
+            pair = apply(power, b * WB, *by)
             if power < 3:
-                keep(power, pl.multiple_of(at + reach, HB), pair)
-            return 0
-
-        lax.fori_loop(0, inner, step, 0, unroll=4)
+                for part in range(2):
+                    place = slice(b * WB + HB, b * WB + HB + WB)
+                    xs[power, part * rows : (part + 1) * rows, place] = pair[part]
+            if 0 < b <= inner:
+                for ref, value in zip((high_ref, low_ref), pair):
+                    ref[power * rows : (power + 1) * rows, b * WB - WB : b * WB] = value
 
     tall = high_ref[...]
     gram = mm(tall, tall, NT) + 2.0 * mm(tall, low_ref[...], NT)
@@ -121,25 +121,22 @@
 
 
 def pack(ref, gram):
-    half = ref.shape[2]
-    part = half // ref.shape[0]
+    half = ref.shape[1]
     across = places(half)
     tail = gram[half:, half:]
-    ref[:, :part] = gram[:half, half:].reshape(-1, part, half)
-    both = jnp.where(across >= 0, gram[:half, :half], tail)
-    ref[:, part : 2 * part] = both.reshape(-1, part, half)
-    ref[:, 2 * part :] = jnp.zeros((ref.shape[0], 8, half), jnp.float32)
+    ref[:half] = gram[:half, half:]
+    ref[half : 2 * half] = jnp.where(across >= 0, gram[:half, :half], tail)
+    ref[2 * half :] = jnp.zeros((ref.shape[0] - 2 * half, half), jnp.float32)
     middle = jnp.sum(jnp.where(across == 0, tail, 0.0), axis=0, keepdims=True)
-    ref[0, 2 * part : 2 * part + 1] = middle
+    ref[2 * half : 2 * half + 1] = middle
 
 
 def unpack(ref):
-    half = ref.shape[2]
-    part = half // ref.shape[0]
+    half = ref.shape[1]
     across = places(half)
-    cross = ref[:, :part].reshape(half, half)
-    both = ref[:, part : 2 * part].reshape(half, half)
-    middle = jnp.broadcast_to(ref[0, 2 * part : 2 * part + 1], (half, half))
+    cross = ref[:half]
+    both = ref[half : 2 * half]
+    middle = jnp.broadcast_to(ref[2 * half : 2 * half + 1], (half, half))
     upper = jnp.where(across > 0, both, 0.0)
     lower = jnp.where(across < 0, both, 0.0)
     head = upper + upper.T + jnp.where(across == 0, both, 0.0)
@@ -213,21 +210,20 @@
     keep = out_ref.shape[0]
     g11, g12, g22 = unpack(gram_ref)
     one = compress(g11, keep, work)
-    mixed = [exact(exact(one, g), one, NT) for g in (g11, g12, g22)]
-    top = jnp.concatenate([mixed[0], mixed[1]], axis=1)
-    bottom = jnp.concatenate([mixed[1].T, mixed[2]], axis=1)
+    cross = exact(exact(one, g12), one, NT)
+    tail = exact(exact(one, g22), one, NT)
+    same = jnp.where(places(keep) == 0, 1.0, 0.0)
+    top = jnp.concatenate([same, cross], axis=1)
+    bottom = jnp.concatenate([cross.T, tail], axis=1)
     two = compress(jnp.concatenate([top, bottom], axis=0), keep, work)
     overall = jnp.concatenate([exact(two[:, :keep], one), exact(two[:, keep:], one)], axis=1)
     fh, fl = split(overall)
     both = jnp.concatenate([fh, fl], axis=0)
 
-    def step(b, _):
-        place = pl.ds(pl.multiple_of(b * WB, WB), WB)
+    for b in range(out_ref.shape[1] // WB):
+        place = slice(b * WB, b * WB + WB)
         wide = mm(both, high_ref[:, place])
         out_ref[:, place] = wide[:keep] + wide[keep:] + mm(fh, low_ref[:, place])
-        return 0
-
-    lax.fori_loop(0, out_ref.shape[1] // WB, step, 0)
 
 
 def exchange(blocks, axis):
@@ -257,7 +253,7 @@
     by_high, by_low = pl.pallas_call(
         blocks_kernel,
         out_shape=[blocks, blocks],
-        scratch_shapes=[pltpu.VMEM((2 * HB, SPAN), jnp.bfloat16)],
+        scratch_shapes=[pltpu.VMEM((2, WB, 3 * HB), jnp.float32)],
         compiler_params=pltpu.CompilerParams(vmem_limit_bytes=12 * 1024 * 1024),
         cost_estimate=pl.CostEstimate(
             flops=10_000_000_000, bytes_accessed=12_000_000, transcendentals=0
@@ -270,7 +266,7 @@
         out_shape=[
             jax.ShapeDtypeStruct((4 * rows, width), jnp.bfloat16),
             jax.ShapeDtypeStruct((4 * rows, width), jnp.bfloat16),
-            jax.ShapeDtypeStruct((group, 4 * rows // group + 8, 2 * rows), jnp.float32),
+            jax.ShapeDtypeStruct((4 * rows + 16, 2 * rows), jnp.float32),
         ],
         scratch_shapes=[
             pltpu.VMEM((3, 2 * rows, wide), jnp.bfloat16),
@@ -281,9 +277,9 @@
         name="powers",
     )(source, low, high, offsets, by_high, by_low)
 
-    gram = exchange(gram, "near").sum(axis=0)
+    gram = exchange(gram.reshape(group, -1, 1, 2 * rows), "near").sum(axis=0)
     gram = copies(gram, "far").sum(axis=0)
-    gram = copies(gram, "near")
+    gram = copies(gram, "near").reshape(4 * rows + 16, 2 * rows)
 
     return pl.pallas_call(
         finish_kernel,

time: 110 us -> 95 us (0.86)
  Pallas kernels: 47.7 us -> 34.8 us
  blocking collectives: 47.7 us -> 45.3 us
    pallas_call x1, Pallas kernels: 13.1 us -> 6.44 us  [body(): pl.pallas_call(functools.partial(powers_kernel, float(width * devices)),...]
    pallas_call x1, Pallas kernels: 8.71 us -> 5.27 us  [body(): pl.pallas_call(blocks_kernel, out_shape=[blocks, blocks], scratch_shapes=...]
    pallas_call x1, Pallas kernels: 25.9 us -> 23.1 us  [body(): pl.pallas_call(finish_kernel, out_shape=jax.ShapeDtypeStruct((2 * rows, w...]
    all_to_all x3, blocking collectives: 47.7 us -> 45.3 us  [exchange(): return lax.all_to_all(blocks, axis, 0, 0, tiled=True)]
  transfers between devices with their start and end apart: 2 -> 2, of which waited for: 0 -> 0; matrix products, arithmetic and copies ran while one was open for 1% -> 1% of each run, Pallas kernels for 8% -> 6%
where the time goes in v3:
time: 95 us; the launch traced here: 94.6 us
  blocking collectives  45.3 us (48%)
  Pallas kernels  34.8 us (37%)
  local copies, waits for them, and re-layouts  7.32 us (8%)
  starting transfers between devices  6.84 us (7%)
    all_to_all x3, blocking collectives, exchange(): return lax.all_to_all(blocks, axis, 0, 0, tiled=True)  45.3 us
    pallas_call x1, Pallas kernels, body(): pl.pallas_call(finish_kernel, out_shape=jax.ShapeDtypeStruct((2 * rows, w...  23.1 us
    pallas_call x1, Pallas kernels, body(): pl.pallas_call(functools.partial(powers_kernel, float(width * devices)),...  6.44 us
    pallas_call x1, Pallas kernels, body(): pl.pallas_call(blocks_kernel, out_shape=[blocks, blocks], scratch_shapes=...  5.27 us
    ppermute x1, starting transfers between devices, body(): lax.ppermute(packed(source[:, width - reach:], band_values[:, width - WB:...  4.92 us
    unnamed x8, local copies, waits for them, and re-layouts  4.49 us
    ppermute x1, starting transfers between devices, body(): lax.ppermute(packed(source[:, :reach], band_values[:, :WB]), ROWS, down)  1.92 us
  transfers between devices with their start and end apart: 2, of which 0 were waited for; matrix products, arithmetic and copies ran while one was open for 1% of the time, Pallas kernels for 6%

profile of v3, /device:TPU:1, one launch (start us, length us, event | category | flops | bytes accessed | tf_op | source)
XLA Modules:
  0.0 94.6 jit_solution(4117132974670890687)
XLA Ops:
  0.0 1.0 %fusion.1 = (f32[64,384]{1,0:T(8,128)S(1)}, f32[64,384]{1,0:T(8,128)S(1)}) fusion(f32[64,4096]{1,0:T(8,128)} %src_ref.1), kind=kLoop, calls=%fused_computation.3 | loop fusion | bytes 393216 | tf_op jit(solution)/shard_map/slice | solution.py:250
  1.0 1.0 %fusion = (f32[64,256]{1,0:T(8,128)S(1)}, f32[64,256]{1,0:T(8,128)S(1)}, f32[64,256]{1,0:T(8,128)S(1)}, f32[64,256]{1,0:T(8,128)S(1)}) fusion(f32[128,4096]{1,0:T(8,128)} %band_ref.1), kind=kLoop, calls=%fused_computation.2 | loop fusion | bytes 524288 | tf_op jit(solution)/shard_map/slice | solution.py:247
  1.9 4.9 %collective-permute-start = (f32[64,896]{1,0:T(8,128)S(1)}, f32[64,896]{1,0:T(8,128)S(1)}, u32[]{:S(2)}, u32[]{:S(2)}) collective-permute-start(f32[64,896]{1,0:T(8,128)S(1)} %pad_maximum_fusion), channel_id=1, source_target_pairs={{0,1},{1,2},{2,3},{3,4},{4,5},{5,6},{6,7},{7,8},{8,9},{9,10},{10,1... | collective-permute-start | bytes 688136 | tf_op jit(solution)/shard_map/ppermute | solution.py:249
  6.9 1.9 %collective-permute-start.1 = (f32[64,896]{1,0:T(8,128)S(1)}, f32[64,896]{1,0:T(8,128)S(1)}, u32[]{:S(2)}, u32[]{:S(2)}) collective-permute-start(f32[64,896]{1,0:T(8,128)S(1)} %pad_maximum_fusion.1), channel_id=1, source_target_pairs={{1,0},{2,1},{3,2},{4,3},{5,4},{6,5},{7,6},{8,7},{9,8},{10,9},{11,1... | collective-permute-start | bytes 688136 | tf_op jit(solution)/shard_map/ppermute | solution.py:250
  8.8 0.8 copy.15.off_ref
  9.6 0.0 copy-start.3
  9.6 1.6 %copy-done.3 = f32[128,4096]{1,0:T(8,128)S(1)} copy-done((f32[128,4096]{1,0:T(8,128)S(1)}, f32[128,4096]{1,0:T(8,128)}, u32[]{:S(2)}) %copy-start.3) | copy-done | bytes 2097176
  11.2 0.0 copy-start.2
  11.2 5.3 %blocks.1 = (bf16[16,512,256]{2,1,0:T(8,128)(2,1)S(1)}, bf16[16,512,256]{2,1,0:T(8,128)(2,1)S(1)}) custom-call(f32[128,4096]{1,0:T(8,128)S(1)} %copy-done.3, s32[128,1]{1,0:T(8,128)S(1)} %copy.15.off_ref), custom_call_target="tpu_custom_call" | custom-call | flops 10000000000 | bytes 12000000 | tf_op jit(solution)/shard_map/blocks/pallas_call | solution.py:253
  16.5 0.0 collective-permute-done.low_in
  16.5 0.0 collective-permute-done.1.high_in
  16.5 0.0 copy-done.2
  16.5 6.4 %powers.1 = (bf16[256,4096]{1,0:T(8,128)(2,1)S(1)}, bf16[256,4096]{1,0:T(8,128)(2,1)S(1)}, f32[272,128]{1,0:T(8,128)S(1)}) custom-call(f32[64,4096]{1,0:T(8,128)S(1)} %copy-done.2, f32[64,896]{1,0:T(8,128)S(1)} %collective-permute-done.low_in, f32[64,896]{1,0:T(8,128)S(1)} %collective-permute-done.1.high_in, s32[128,1]{1,0:T(8,128)S(1)} %copy.15.off_ref, ...), custom_call_target="tpu_custom_call" | custom-call | tf_op jit(solution)/shard_map/powers/pallas_call | solution.py:264
  22.9 0.0 copy-start
  23.0 1.3 %copy-done = bf16[256,4096]{1,0:T(8,128)(2,1)} copy-done((bf16[256,4096]{1,0:T(8,128)(2,1)}, bf16[256,4096]{1,0:T(8,128)(2,1)S(1)}, u32[]{:S(2)}) %copy-start) | copy-done | bytes 2097176
  24.3 18.7 %all_to_all.15 = f32[16,17,1,128]{3,2,1,0:T(1,128)S(1)} all-to-all(f32[16,17,1,128]{3,2,1,0:T(1,128)S(1)} %bitcast.4), channel_id=1, replica_groups=mesh['far'=16,'near'=16] {'near'}, dimensions={0} | all-to-all | bytes 278528 | tf_op jit(solution)/shard_map/all_to_all | solution.py:230
  43.0 0.1 reduce_sum.18
  43.1 0.1 broadcast_in_dim.6
  43.2 13.9 %all_to_all.16 = f32[16,17,1,128]{3,2,1,0:T(1,128)S(1)} all-to-all(f32[16,17,1,128]{3,2,1,0:T(1,128)S(1)} %broadcast_in_dim.6), channel_id=1, replica_groups=mesh['far'=16,'near'=16] {'far'}, dimensions={0} | all-to-all | bytes 278528 | tf_op jit(solution)/shard_map/all_to_all | solution.py:230
  57.1 0.1 reduce_sum.19
  57.2 0.1 broadcast_in_dim.7
  57.3 12.7 %all_to_all.17 = f32[16,17,1,128]{3,2,1,0:T(1,128)S(1)} all-to-all(f32[16,17,1,128]{3,2,1,0:T(1,128)S(1)} %broadcast_in_dim.7), channel_id=1, replica_groups=mesh['far'=16,'near'=16] {'near'}, dimensions={0} | all-to-all | bytes 278528 | tf_op jit(solution)/shard_map/all_to_all | solution.py:230
  70.0 1.6 %copy-done.1 = bf16[256,4096]{1,0:T(8,128)(2,1)S(1)} copy-done((bf16[256,4096]{1,0:T(8,128)(2,1)S(1)}, bf16[256,4096]{1,0:T(8,128)(2,1)}, u32[]{:S(2)}) %copy-start.1) | copy-done | bytes 2097176
  71.6 23.1 %finish.1 = f32[128,4096]{1,0:T(8,128)} custom-call(f32[272,128]{1,0:T(8,128)S(1)} %bitcast.3, bf16[256,4096]{1,0:T(8,128)(2,1)S(1)} %get-tuple-element.13.high_ref, bf16[256,4096]{1,0:T(8,128)(2,1)S(1)} %copy-done.1), custom_call_target="tpu_custom_call" | custom-call | tf_op jit(solution)/shard_map/finish/pallas_call | solution.py:284
  (3 shorter events, 0.0 us)
Async XLA Ops:
  1.9 14.5 %collective-permute-start = (f32[64,896]{1,0:T(8,128)S(1)}, f32[64,896]{1,0:T(8,128)S(1)}, u32[]{:S(2)}, u32[]{:S(2)}) collective-permute-start(f32[64,896]{1,0:T(8,128)S(1)} %pad_maximum_fusion), channel_id=1, source_target_pairs={{0,1},{1,2},{2,3},{3,4},{4,5},{5,6},{6,7},{7,8},{8,9},{9,10},{10,1... | collective-permute-start | bytes 688136 | tf_op jit(solution)/shard_map/ppermute | solution.py:249
  6.9 9.6 %collective-permute-start.1 = (f32[64,896]{1,0:T(8,128)S(1)}, f32[64,896]{1,0:T(8,128)S(1)}, u32[]{:S(2)}, u32[]{:S(2)}) collective-permute-start(f32[64,896]{1,0:T(8,128)S(1)} %pad_maximum_fusion.1), channel_id=1, source_target_pairs={{1,0},{2,1},{3,2},{4,3},{5,4},{6,5},{7,6},{8,7},{9,8},{10,9},{11,1... | collective-permute-start | bytes 688136 | tf_op jit(solution)/shard_map/ppermute | solution.py:250
  9.6 1.6 %copy-start.3 = (f32[128,4096]{1,0:T(8,128)S(1)}, f32[128,4096]{1,0:T(8,128)}, u32[]{:S(2)}) copy-start(f32[128,4096]{1,0:T(8,128)} %band_ref.1) | copy-start | bytes 6291460
  11.2 5.3 %copy-start.2 = (f32[64,4096]{1,0:T(8,128)S(1)}, f32[64,4096]{1,0:T(8,128)}, u32[]{:S(2)}) copy-start(f32[64,4096]{1,0:T(8,128)} %src_ref.1) | copy-start | bytes 3145732
  22.9 1.3 %copy-start = (bf16[256,4096]{1,0:T(8,128)(2,1)}, bf16[256,4096]{1,0:T(8,128)(2,1)S(1)}, u32[]{:S(2)}) copy-start(bf16[256,4096]{1,0:T(8,128)(2,1)S(1)} %get-tuple-element.14.low_ref) | copy-start | bytes 6291460
  70.0 1.6 %copy-start.1 = (bf16[256,4096]{1,0:T(8,128)(2,1)S(1)}, bf16[256,4096]{1,0:T(8,128)(2,1)}, u32[]{:S(2)}) copy-start(bf16[256,4096]{1,0:T(8,128)(2,1)} %copy-done) | copy-start | bytes 6291460

commit v4 on v3

--- a/solution.py
+++ b/solution.py
@@ -32,13 +32,13 @@
 
 
 def picker(off_ref):
-    lanes = lax.broadcasted_iota(jnp.int32, (off_ref.shape[0], 3 * HB), 1)
-    pick = jnp.where(lanes == off_ref[...] + HB, 1.0, 0.0).astype(jnp.bfloat16)
-    return jnp.concatenate([pick, pick], axis=0)
+    down = lax.broadcasted_iota(jnp.int32, (3 * HB, off_ref.shape[1]), 0)
+    pick = jnp.where(down == off_ref[...] + HB, 1.0, 0.0).astype(jnp.bfloat16)
+    return jnp.concatenate([pick, pick], axis=1)
 
 
 def diagonals(values, pick):
-    return mm(jnp.concatenate(split(values.T), axis=1), pick)
+    return mm(jnp.concatenate(split(values.T), axis=1), pick, NT)
 
 
 def place_block(diag, wh, wl, b):
@@ -60,6 +60,23 @@
             diag_ref[b % 2] = diagonals(band_ref[:, b * WB : b * WB + WB], pick)
         if b > 0:
             place_block(diag_ref[(b - 1) % 2], wh, wl, b - 1)
+
+
+def edges_kernel(src_ref, band_ref, up_ref, down_ref, sems):
+    rows, width = src_ref.shape
+    reach = 3 * HB
+    copies = []
+    for ref, far, near in ((up_ref, width - reach, width - WB), (down_ref, 0, 0)):
+        parts = [(src_ref.at[:, pl.ds(far, reach)], ref.at[:, pl.ds(0, reach)])]
+        for half in range(2):
+            take = band_ref.at[pl.ds(half * rows, rows), pl.ds(near, WB)]
+            parts.append((take, ref.at[:, pl.ds(reach + half * WB, WB)]))
+        for one, two in parts:
+            copies.append(pltpu.make_async_copy(one, two, sems.at[len(copies)]))
+    for copy in copies:
+        copy.start()
+    for copy in copies:
+        copy.wait()
 
 
 def powers_kernel(
@@ -108,7 +125,6 @@
             if 0 < b <= inner:
                 for ref, value in zip((high_ref, low_ref), pair):
                     ref[power * rows : (power + 1) * rows, b * WB - WB : b * WB] = value
-
     tall = high_ref[...]
     gram = mm(tall, tall, NT) + 2.0 * mm(tall, low_ref[...], NT)
     pack(gram_ref, (gram + gram.T) * (0.5 / total))
@@ -192,46 +208,66 @@
                 work[tile(g, t)] = rest[t]
 
 
-def compress(gram, retain, work):
-    order = gram.shape[0]
-    spanning = gram[:retain]
-    for turn in range(2):
-        if turn > 0:
-            spanning = exact(work[:, retain : retain + order], gram)
-        mapped = exact(spanning, gram)
-        metric = exact(mapped, spanning, NT)
-        work[:, :retain] = 0.5 * (metric + metric.T)
-        work[:, retain : retain + order] = spanning
-        eliminate(work, (retain + order) // 128)
+def compress(gram, spanning, work):
+    retain, order = spanning.shape
+    metric = exact(exact(spanning, gram), spanning, NT)
+    work[:, :retain] = 0.5 * (metric + metric.T)
+    work[:, retain : retain + order] = spanning
+    eliminate(work, (retain + order) // 128)
     return work[:, retain : retain + order]
 
 
-def finish_kernel(gram_ref, high_ref, low_ref, out_ref, work):
+def finish_kernel(gram_ref, high_ref, low_ref, out_ref, work, out, sems):
     keep = out_ref.shape[0]
     g11, g12, g22 = unpack(gram_ref)
-    one = compress(g11, keep, work)
+    one = compress(g11, g11, work)
+    one = compress(g11, exact(one, g11), work)
     cross = exact(exact(one, g12), one, NT)
     tail = exact(exact(one, g22), one, NT)
     same = jnp.where(places(keep) == 0, 1.0, 0.0)
     top = jnp.concatenate([same, cross], axis=1)
     bottom = jnp.concatenate([cross.T, tail], axis=1)
-    two = compress(jnp.concatenate([top, bottom], axis=0), keep, work)
+    gram = jnp.concatenate([top, bottom], axis=0)
+    two = compress(gram, exact(top, gram), work)
     overall = jnp.concatenate([exact(two[:, :keep], one), exact(two[:, keep:], one)], axis=1)
     fh, fl = split(overall)
     both = jnp.concatenate([fh, fl], axis=0)
 
-    for b in range(out_ref.shape[1] // WB):
+    quarter = out.shape[1] // 4
+    stores = []
+    for b in range(out.shape[1] // WB):
         place = slice(b * WB, b * WB + WB)
         wide = mm(both, high_ref[:, place])
-        out_ref[:, place] = wide[:keep] + wide[keep:] + mm(fh, low_ref[:, place])
+        out[:, place] = wide[:keep] + wide[keep:] + mm(fh, low_ref[:, place])
+        if (b + 1) * WB % quarter == 0:
+            at = pl.ds((b + 1) * WB - quarter, quarter)
+            sem = sems.at[len(stores)]
+            stores.append(pltpu.make_async_copy(out.at[:, at], out_ref.at[:, at], sem))
+            stores[-1].start()
+    for store in stores:
+        store.wait()
+
+
+def sum_kernel(in_ref, out_ref):
+    total = in_ref[0]
+    for i in range(1, in_ref.shape[0]):
+        total = total + in_ref[i]
+    for i in range(out_ref.shape[0]):
+        out_ref[i] = total
 
 
 def exchange(blocks, axis):
     return lax.all_to_all(blocks, axis, 0, 0, tiled=True)
 
 
-def copies(x, axis):
-    return exchange(jnp.broadcast_to(x, (lax.axis_size(axis), *x.shape)), axis)
+def summed_copies(blocks, axis):
+    copies = pl.pallas_call(
+        sum_kernel,
+        out_shape=jax.ShapeDtypeStruct((lax.axis_size(axis), *blocks.shape[1:]), jnp.float32),
+        compiler_params=pltpu.CompilerParams(vmem_limit_bytes=8 * 1024 * 1024),
+        name="sums_" + axis,
+    )(blocks)
+    return exchange(copies, axis)
 
 
 def body(source, band_values, offsets):
@@ -243,12 +279,20 @@
     up = [(i, i + 1) for i in range(devices - 1)]
     down = [(i + 1, i) for i in range(devices - 1)]
 
-    def packed(far, near):
-        return jnp.concatenate([far, near[:rows], near[rows:]], axis=1)
-
-    low = lax.ppermute(packed(source[:, width - reach :], band_values[:, width - WB :]), ROWS, up)
-    high = lax.ppermute(packed(source[:, :reach], band_values[:, :WB]), ROWS, down)
-    offsets = offsets.reshape(-1, 1)
+    hbm = pl.BlockSpec(memory_space=pltpu.HBM)
+    vmem = pl.BlockSpec(memory_space=pltpu.VMEM)
+    edge = jax.ShapeDtypeStruct((rows, reach + 2 * WB), jnp.float32)
+    last, first = pl.pallas_call(
+        edges_kernel,
+        out_shape=[edge, edge],
+        in_specs=[hbm, hbm],
+        scratch_shapes=[pltpu.SemaphoreType.DMA((6,))],
+        compiler_params=pltpu.CompilerParams(vmem_limit_bytes=64_500_000),
+        name="edges",
+    )(source, band_values)
+    low = lax.ppermute(last, ROWS, up)
+    high = lax.ppermute(first, ROWS, down)
+    offsets = offsets.reshape(1, -1)
     blocks = jax.ShapeDtypeStruct((inner, SPAN, WB), jnp.bfloat16)
     by_high, by_low = pl.pallas_call(
         blocks_kernel,
@@ -277,14 +321,19 @@
         name="powers",
     )(source, low, high, offsets, by_high, by_low)
 
-    gram = exchange(gram.reshape(group, -1, 1, 2 * rows), "near").sum(axis=0)
-    gram = copies(gram, "far").sum(axis=0)
-    gram = copies(gram, "near").reshape(4 * rows + 16, 2 * rows)
+    gram = exchange(gram.reshape(group, -1, 1, 2 * rows), "near")
+    gram = summed_copies(summed_copies(gram, "far"), "near")
+    gram = gram.reshape(4 * rows + 16, 2 * rows)
 
     return pl.pallas_call(
         finish_kernel,
         out_shape=jax.ShapeDtypeStruct((2 * rows, width), jnp.float32),
-        scratch_shapes=[pltpu.VMEM((2 * rows, 6 * rows), jnp.float32)],
+        out_specs=hbm,
+        scratch_shapes=[
+            pltpu.VMEM((2 * rows, 6 * rows), jnp.float32),
+            pltpu.VMEM((2 * rows, width), jnp.float32),
+            pltpu.SemaphoreType.DMA((4,)),
+        ],
         compiler_params=pltpu.CompilerParams(vmem_limit_bytes=16 * 1024 * 1024),
         name="finish",
     )(gram, high, low)

time: 95 us -> 84.2 us (0.89)
  local copies, waits for them, and re-layouts: 7.32 us -> 0.01 us
  Pallas kernels: 34.8 us -> 31.5 us
    pallas_call x1, Pallas kernels: 23.1 us -> 17.5 us  [body(): pl.pallas_call(finish_kernel, out_shape=jax.ShapeDtypeStruct((2 * rows, w...]
    unnamed x8 -> x6, local copies, waits for them, and re-layouts: 4.49 us -> 0.01 us
    pallas_call x0 -> x3, Pallas kernels: none -> 2.19 us  [the longest x1 1.99 us: body(): pl.pallas_call(edges_kernel, out_shape=[edge, edge], in_specs=[hbm, hbm],...]
    slice x2 -> x0, local copies, waits for them, and re-layouts: 1.91 us -> none  [the longest x1 0.96 us: packed(): return jnp.concatenate([far, near[:rows], near[rows:]], axis=1)]
  transfers between devices with their start and end apart: 2 -> 2, of which waited for: 0 -> 1; matrix products, arithmetic and copies ran while one was open for 1% -> 0% of each run, Pallas kernels for 6% -> 6%
where the time goes in v4:
time: 84.2 us; the launch traced here: 83.9 us
  blocking collectives  45.1 us (54%)
  Pallas kernels  31.5 us (37%)
  starting transfers between devices  6.84 us (8%)
    all_to_all x3, blocking collectives, exchange(): return lax.all_to_all(blocks, axis, 0, 0, tiled=True)  45.1 us
    pallas_call x1, Pallas kernels, body(): pl.pallas_call(finish_kernel, out_shape=jax.ShapeDtypeStruct((2 * rows, w...  17.5 us
    pallas_call x1, Pallas kernels, body(): pl.pallas_call(functools.partial(powers_kernel, float(width * devices)),...  6.46 us
    pallas_call x1, Pallas kernels, body(): pl.pallas_call(blocks_kernel, out_shape=[blocks, blocks], scratch_shapes=...  5.27 us
    ppermute x1, starting transfers between devices, body(): low = lax.ppermute(last, ROWS, up)  4.92 us
    pallas_call x1, Pallas kernels, body(): pl.pallas_call(edges_kernel, out_shape=[edge, edge], in_specs=[hbm, hbm],...  1.99 us
    ppermute x1, starting transfers between devices, body(): high = lax.ppermute(first, ROWS, down)  1.92 us
  transfers between devices with their start and end apart: 2, of which 1 were waited for; matrix products, arithmetic and copies ran while one was open for 0% of the time, Pallas kernels for 6%

profile of v4, /device:TPU:1, one launch (start us, length us, event | category | flops | bytes accessed | tf_op | source)
XLA Modules:
  0.0 83.9 jit_solution(8278163304954718977)
XLA Ops:
  0.0 0.0 copy-start.1
  0.0 0.0 copy-start.2
  0.0 2.0 %edges.1 = (f32[64,896]{1,0:T(8,128)}, f32[64,896]{1,0:T(8,128)}) custom-call(f32[64,4096]{1,0:T(8,128)} %src_ref.3, f32[128,4096]{1,0:T(8,128)} %band_ref.3), custom_call_target="tpu_custom_call" | custom-call | tf_op jit(solution)/shard_map/edges/pallas_call | solution.py:285
  2.0 4.9 %collective-permute-start = (f32[64,896]{1,0:T(8,128)}, f32[64,896]{1,0:T(8,128)S(1)}, u32[]{:S(2)}, u32[]{:S(2)}) collective-permute-start(f32[64,896]{1,0:T(8,128)} %get-tuple-element.12), channel_id=1, source_target_pairs={{0,1},{1,2},{2,3},{3,4},{4,5},{5,6},{6,7},{7,8},{8,9},{9,10},{10,1... | collective-permute-start | bytes 688136 | tf_op jit(solution)/shard_map/ppermute | solution.py:293
  6.9 1.9 %collective-permute-start.1 = (f32[64,896]{1,0:T(8,128)}, f32[64,896]{1,0:T(8,128)S(1)}, u32[]{:S(2)}, u32[]{:S(2)}) collective-permute-start(f32[64,896]{1,0:T(8,128)} %get-tuple-element.13), channel_id=1, source_target_pairs={{1,0},{2,1},{3,2},{4,3},{5,4},{6,5},{7,6},{8,7},{9,8},{10,9},{11,1... | collective-permute-start | bytes 688136 | tf_op jit(solution)/shard_map/ppermute | solution.py:294
  8.9 0.0 copy-done.1
  8.9 0.0 copy-done.2
  8.9 0.0 copy-start
  8.9 5.3 %blocks.1 = (bf16[16,512,256]{2,1,0:T(8,128)(2,1)S(1)}, bf16[16,512,256]{2,1,0:T(8,128)(2,1)S(1)}) custom-call(f32[128,4096]{1,0:T(8,128)S(1)} %copy-done.1, s32[1,128]{1,0:T(1,128)S(1)} %bitcast.5), custom_call_target="tpu_custom_call" | custom-call | flops 10000000000 | bytes 12000000 | tf_op jit(solution)/shard_map/blocks/pallas_call | solution.py:297
  14.2 0.0 collective-permute-done.low_in
  14.2 0.3 collective-permute-done.1.high_in
  14.5 0.0 copy-done
  14.5 6.5 %powers.1 = (bf16[256,4096]{1,0:T(8,128)(2,1)S(1)}, bf16[256,4096]{1,0:T(8,128)(2,1)S(1)}, f32[272,128]{1,0:T(8,128)S(1)}) custom-call(f32[64,4096]{1,0:T(8,128)S(1)} %copy-done, f32[64,896]{1,0:T(8,128)S(1)} %collective-permute-done.low_in, f32[64,896]{1,0:T(8,128)S(1)} %collective-permute-done.1.high_in, s32[1,128]{1,0:T(1,128)S(1)} %bitcast.6, ...), custom_call_target="tpu_custom_call" | custom-call | tf_op jit(solution)/shard_map/powers/pallas_call | solution.py:308
  21.0 18.5 %all_to_all.15.in_ref = f32[16,17,1,128]{3,2,1,0:T(1,128)S(1)} all-to-all(f32[16,17,1,128]{3,2,1,0:T(1,128)S(1)} %bitcast.4), channel_id=1, replica_groups=mesh['far'=16,'near'=16] {'near'}, dimensions={0} | all-to-all | bytes 278528 | tf_op jit(solution)/shard_map/all_to_all | solution.py:260
  39.4 0.1 sums_far.1
  39.5 13.9 %all_to_all.16.in_ref = f32[16,17,1,128]{3,2,1,0:T(1,128)S(1)} all-to-all(f32[16,17,1,128]{3,2,1,0:T(1,128)S(1)} %sums_far.1), channel_id=1, replica_groups=mesh['far'=16,'near'=16] {'far'}, dimensions={0} | all-to-all | bytes 278528 | tf_op jit(solution)/shard_map/all_to_all | solution.py:260
  53.4 0.1 sums_near.1
  53.5 12.7 %all_to_all.17 = f32[16,17,1,128]{3,2,1,0:T(1,128)S(1)} all-to-all(f32[16,17,1,128]{3,2,1,0:T(1,128)S(1)} %sums_near.1), channel_id=1, replica_groups=mesh['far'=16,'near'=16] {'near'}, dimensions={0} | all-to-all | bytes 278528 | tf_op jit(solution)/shard_map/all_to_all | solution.py:260
  66.2 17.5 %finish.1 = f32[128,4096]{1,0:T(8,128)} custom-call(f32[272,128]{1,0:T(8,128)S(1)} %bitcast.3, bf16[256,4096]{1,0:T(8,128)(2,1)S(1)} %get-tuple-element.17.high_ref, bf16[256,4096]{1,0:T(8,128)(2,1)S(1)} %get-tuple-element.18.low_ref), custom_call_target="tpu_custom_call" | custom-call | tf_op jit(solution)/shard_map/finish/pallas_call | solution.py:328
Async XLA Ops:
  0.0 8.9 %copy-start.1 = (f32[128,4096]{1,0:T(8,128)S(1)}, f32[128,4096]{1,0:T(8,128)}, u32[]{:S(2)}) copy-start(f32[128,4096]{1,0:T(8,128)} %band_ref.3) | copy-start | bytes 6291460
  0.0 8.9 %copy-start.2 = (s32[128]{0:T(128)S(1)}, s32[128]{0:T(128)}, u32[]{:S(2)}) copy-start(s32[128]{0:T(128)} %param.5) | copy-start | bytes 1540
  2.0 12.2 %collective-permute-start = (f32[64,896]{1,0:T(8,128)}, f32[64,896]{1,0:T(8,128)S(1)}, u32[]{:S(2)}, u32[]{:S(2)}) collective-permute-start(f32[64,896]{1,0:T(8,128)} %get-tuple-element.12), channel_id=1, source_target_pairs={{0,1},{1,2},{2,3},{3,4},{4,5},{5,6},{6,7},{7,8},{8,9},{9,10},{10,1... | collective-permute-start | bytes 688136 | tf_op jit(solution)/shard_map/ppermute | solution.py:293
  6.9 7.5 %collective-permute-start.1 = (f32[64,896]{1,0:T(8,128)}, f32[64,896]{1,0:T(8,128)S(1)}, u32[]{:S(2)}, u32[]{:S(2)}) collective-permute-start(f32[64,896]{1,0:T(8,128)} %get-tuple-element.13), channel_id=1, source_target_pairs={{1,0},{2,1},{3,2},{4,3},{5,4},{6,5},{7,6},{8,7},{9,8},{10,9},{11,1... | collective-permute-start | bytes 688136 | tf_op jit(solution)/shard_map/ppermute | solution.py:294
  8.9 5.6 %copy-start = (f32[64,4096]{1,0:T(8,128)S(1)}, f32[64,4096]{1,0:T(8,128)}, u32[]{:S(2)}) copy-start(f32[64,4096]{1,0:T(8,128)} %src_ref.3) | copy-start | bytes 3145732

commit v5 on v4

--- a/solution.py
+++ b/solution.py
@@ -32,34 +32,67 @@
 
 
 def picker(off_ref):
-    down = lax.broadcasted_iota(jnp.int32, (3 * HB, off_ref.shape[1]), 0)
+    count = off_ref.shape[1]
+    down = lax.broadcasted_iota(jnp.int32, (2 * HB, count), 0)
     pick = jnp.where(down == off_ref[...] + HB, 1.0, 0.0).astype(jnp.bfloat16)
-    return jnp.concatenate([pick, pick], axis=1)
-
-
-def diagonals(values, pick):
-    return mm(jnp.concatenate(split(values.T), axis=1), pick, NT)
-
-
-def place_block(diag, wh, wl, b):
+    last = jnp.where(off_ref[...] == HB, 1.0, 0.0)
+    last = jnp.sum(jnp.where(places(count) == 0, last, 0.0), axis=1, keepdims=True)
+    return jnp.concatenate([pick, pick], axis=1), last
+
+
+def turned(values):
+    return jnp.concatenate(split(values.T), axis=1)
+
+
+def quarters():
+    for half in range(2):
+        for t in range(2):
+            yield slice(half * HB, half * HB + HB), slice(t * HB, t * HB + HB)
+
+
+def skew(diag, ref):
+    for rows, lanes in quarters():
+        ref[rows, lanes] = pltpu.roll(diag[rows, lanes], 0, 1, stride=1, stride_axis=0)
+
+
+def place_block(rolled, last, wh, wl, b):
+    beyond = places(HB)
+    parts = [rolled[rows, lanes].T for rows, lanes in quarters()]
     for half in range(2):
         rows = slice(half * HB, half * HB + HB)
-        band = pltpu.roll(diag[rows], 0, 1, stride=1, stride_axis=0)
-        high, low = split(band.T)
-        for ref, part in ((wh, high), (wl, low)):
-            ref[b, half * HB : half * HB + 3 * HB, rows] = part
-            empty = 3 * HB * (1 - half)
+        near, far = parts[2 * half : 2 * half + 2]
+        edge = jnp.where(beyond == 0, last[:, rows], 0.0)
+        tiles = [
+            jnp.where(beyond <= 0, near, 0.0),
+            jnp.where(beyond <= 0, far, near),
+            jnp.where(beyond > 0, far, edge),
+        ]
+        for t, tile in enumerate(tiles):
+            high, low = split(tile)
+            for ref, part in ((wh, high), (wl, low)):
+                ref[b, (half + t) * HB : (half + t + 1) * HB, rows] = part
+        empty = 3 * HB * (1 - half)
+        for ref in (wh, wl):
             ref[b, empty : empty + HB, rows] = jnp.zeros((HB, HB), jnp.bfloat16)
 
 
-def blocks_kernel(band_ref, off_ref, wh, wl, diag_ref):
-    pick = picker(off_ref)
+def final(values, last):
+    return jnp.sum(values * last, axis=0, keepdims=True)
+
+
+def blocks_kernel(band_ref, off_ref, wh, wl, both_ref, diag_ref, rolled_ref):
+    pick, last = picker(off_ref)
     count = wh.shape[0]
-    for b in range(count + 1):
+    for b in range(count + 3):
+        if b >= 3:
+            values = band_ref[:, (b - 3) * WB : (b - 2) * WB]
+            place_block(rolled_ref[(b - 3) % 2], final(values, last), wh, wl, b - 3)
+        if 2 <= b < count + 2:
+            skew(diag_ref[(b - 2) % 2], rolled_ref.at[(b - 2) % 2])
+        if 1 <= b < count + 1:
+            diag_ref[(b - 1) % 2] = mm(both_ref[(b - 1) % 2], pick, NT)
         if b < count:
-            diag_ref[b % 2] = diagonals(band_ref[:, b * WB : b * WB + WB], pick)
-        if b > 0:
-            place_block(diag_ref[(b - 1) % 2], wh, wl, b - 1)
+            both_ref[b % 2] = turned(band_ref[:, b * WB : b * WB + WB])
 
 
 def edges_kernel(src_ref, band_ref, up_ref, down_ref, sems):
@@ -80,7 +113,7 @@
 
 
 def powers_kernel(
-    total, src_ref, low_in, high_in, off_ref, wh, wl, high_ref, low_ref, gram_ref, xs, eh, el
+    total, src_ref, low_in, high_in, off_ref, wh, wl, high_ref, low_ref, gram_ref, xs, eh, el, rolled
 ):
     rows, width = src_ref.shape
     inner = width // WB
@@ -94,13 +127,18 @@
         low_ref[:rows, at] = low
         xs[0, :rows, into] = high
         xs[0, rows:, into] = low
-    pick = picker(off_ref)
+    pick, last = picker(off_ref)
+    sides = []
     for ref, side, at in edges:
         high, low = split(ref[:, :reach])
         xs[0, :rows, at : at + reach] = high
         xs[0, rows:, at : at + reach] = low
         values = jnp.concatenate([ref[:, reach : reach + WB], ref[:, reach + WB :]], axis=0)
-        place_block(diagonals(values, pick), eh, el, side)
+        sides.append((values, mm(turned(values), pick, NT)))
+    for side, (values, diag) in enumerate(sides):
+        skew(diag, rolled.at[side])
+    for side, (values, diag) in enumerate(sides):
+        place_block(rolled[side], final(values, last), eh, el, side)
     for power in (1, 2):
         for at in (0, xs.shape[2] - HB):
             xs[power, :, at : at + HB] = jnp.zeros((2 * rows, HB), jnp.bfloat16)
@@ -297,7 +335,11 @@
     by_high, by_low = pl.pallas_call(
         blocks_kernel,
         out_shape=[blocks, blocks],
-        scratch_shapes=[pltpu.VMEM((2, WB, 3 * HB), jnp.float32)],
+        scratch_shapes=[
+            pltpu.VMEM((2, WB, 2 * HB), jnp.bfloat16),
+            pltpu.VMEM((2, WB, 2 * HB), jnp.float32),
+            pltpu.VMEM((2, WB, 2 * HB), jnp.float32),
+        ],
         compiler_params=pltpu.CompilerParams(vmem_limit_bytes=12 * 1024 * 1024),
         cost_estimate=pl.CostEstimate(
             flops=10_000_000_000, bytes_accessed=12_000_000, transcendentals=0
@@ -316,6 +358,7 @@
             pltpu.VMEM((3, 2 * rows, wide), jnp.bfloat16),
             pltpu.VMEM((2, SPAN, WB), jnp.bfloat16),
             pltpu.VMEM((2, SPAN, WB), jnp.bfloat16),
+            pltpu.VMEM((2, WB, 2 * HB), jnp.float32),
         ],
         compiler_params=pltpu.CompilerParams(vmem_limit_bytes=16 * 1024 * 1024),
         name="powers",

time: 84.2 us -> 83.2 us (0.988)
  Pallas kernels: 31.5 us -> 29.3 us
  waiting for transfers between devices: 0.31 us -> 1.99 us
    pallas_call x1, Pallas kernels: 5.27 us -> 3.58 us  [body(): pl.pallas_call(blocks_kernel, out_shape=[blocks, blocks], scratch_shapes=...]
    ppermute x1, waiting for transfers between devices: 0.31 us -> 1.99 us  [body(): high = lax.ppermute(first, ROWS, down)]
  transfers between devices with their start and end apart: 2 -> 2, of which waited for: 1 -> 1; matrix products, arithmetic and copies ran while one was open for 0% -> 0% of each run, Pallas kernels for 6% -> 4%
where the time goes in v5:
time: 83.2 us; the launch traced here: 82.9 us
  blocking collectives  44.5 us (53%)
  Pallas kernels  29.3 us (35%)
  starting transfers between devices  6.84 us (8%)
  waiting for transfers between devices  1.99 us (2%)
    all_to_all x3, blocking collectives, exchange(): return lax.all_to_all(blocks, axis, 0, 0, tiled=True)  44.5 us
    pallas_call x1, Pallas kernels, body(): pl.pallas_call(finish_kernel, out_shape=jax.ShapeDtypeStruct((2 * rows, w...  17.5 us
    pallas_call x1, Pallas kernels, body(): pl.pallas_call(functools.partial(powers_kernel, float(width * devices)),...  6.03 us
    ppermute x1, starting transfers between devices, body(): low = lax.ppermute(last, ROWS, up)  4.92 us
    pallas_call x1, Pallas kernels, body(): pl.pallas_call(blocks_kernel, out_shape=[blocks, blocks], scratch_shapes=...  3.58 us
    pallas_call x1, Pallas kernels, body(): pl.pallas_call(edges_kernel, out_shape=[edge, edge], in_specs=[hbm, hbm],...  1.99 us
    ppermute x1, waiting for transfers between devices, body(): high = lax.ppermute(first, ROWS, down)  1.99 us
    ppermute x1, starting transfers between devices, body(): high = lax.ppermute(first, ROWS, down)  1.92 us
  transfers between devices with their start and end apart: 2, of which 1 were waited for; matrix products, arithmetic and copies ran while one was open for 0% of the time, Pallas kernels for 4%

profile of v5, /device:TPU:1, one launch (start us, length us, event | category | flops | bytes accessed | tf_op | source)
XLA Modules:
  0.0 82.9 jit_solution(5366454368817942557)
XLA Ops:
  0.0 0.0 copy-start.1
  0.0 0.0 copy-start.2
  0.0 2.0 %edges.1 = (f32[64,896]{1,0:T(8,128)}, f32[64,896]{1,0:T(8,128)}) custom-call(f32[64,4096]{1,0:T(8,128)} %src_ref.3, f32[128,4096]{1,0:T(8,128)} %band_ref.3), custom_call_target="tpu_custom_call" | custom-call | tf_op jit(solution)/shard_map/edges/pallas_call | solution.py:323
  2.0 4.9 %collective-permute-start = (f32[64,896]{1,0:T(8,128)}, f32[64,896]{1,0:T(8,128)S(1)}, u32[]{:S(2)}, u32[]{:S(2)}) collective-permute-start(f32[64,896]{1,0:T(8,128)} %get-tuple-element.12), channel_id=1, source_target_pairs={{0,1},{1,2},{2,3},{3,4},{4,5},{5,6},{6,7},{7,8},{8,9},{9,10},{10,1... | collective-permute-start | bytes 688136 | tf_op jit(solution)/shard_map/ppermute | solution.py:331
  6.9 1.9 %collective-permute-start.1 = (f32[64,896]{1,0:T(8,128)}, f32[64,896]{1,0:T(8,128)S(1)}, u32[]{:S(2)}, u32[]{:S(2)}) collective-permute-start(f32[64,896]{1,0:T(8,128)} %get-tuple-element.13), channel_id=1, source_target_pairs={{1,0},{2,1},{3,2},{4,3},{5,4},{6,5},{7,6},{8,7},{9,8},{10,9},{11,1... | collective-permute-start | bytes 688136 | tf_op jit(solution)/shard_map/ppermute | solution.py:332
  8.9 0.0 copy-done.1
  8.9 0.0 copy-done.2
  8.9 0.0 copy-start
  8.9 3.6 %blocks.1 = (bf16[16,512,256]{2,1,0:T(8,128)(2,1)S(1)}, bf16[16,512,256]{2,1,0:T(8,128)(2,1)S(1)}) custom-call(f32[128,4096]{1,0:T(8,128)S(1)} %copy-done.1, s32[1,128]{1,0:T(1,128)S(1)} %bitcast.5), custom_call_target="tpu_custom_call" | custom-call | flops 10000000000 | bytes 12000000 | tf_op jit(solution)/shard_map/blocks/pallas_call | solution.py:335
  12.5 0.0 collective-permute-done.low_in
  12.5 2.0 %collective-permute-done.1.high_in = f32[64,896]{1,0:T(8,128)S(1)} collective-permute-done((f32[64,896]{1,0:T(8,128)}, f32[64,896]{1,0:T(8,128)S(1)}, u32[]{:S(2)}, u32[]{:S(2)}) %collective-permute-start.1) | collective-permute-done | bytes 229408 | tf_op jit(solution)/shard_map/ppermute | solution.py:332
  14.5 0.0 copy-done
  14.5 6.0 %powers.1 = (bf16[256,4096]{1,0:T(8,128)(2,1)S(1)}, bf16[256,4096]{1,0:T(8,128)(2,1)S(1)}, f32[272,128]{1,0:T(8,128)S(1)}) custom-call(f32[64,4096]{1,0:T(8,128)S(1)} %copy-done, f32[64,896]{1,0:T(8,128)S(1)} %collective-permute-done.low_in, f32[64,896]{1,0:T(8,128)S(1)} %collective-permute-done.1.high_in, s32[1,128]{1,0:T(1,128)S(1)} %bitcast.6, ...), custom_call_target="tpu_custom_call" | custom-call | tf_op jit(solution)/shard_map/powers/pallas_call | solution.py:350
  20.5 17.3 %all_to_all.15.in_ref = f32[16,17,1,128]{3,2,1,0:T(1,128)S(1)} all-to-all(f32[16,17,1,128]{3,2,1,0:T(1,128)S(1)} %bitcast.4), channel_id=1, replica_groups=mesh['far'=16,'near'=16] {'near'}, dimensions={0} | all-to-all | bytes 278528 | tf_op jit(solution)/shard_map/all_to_all | solution.py:298
  37.8 0.1 sums_far.1
  37.9 14.5 %all_to_all.16.in_ref = f32[16,17,1,128]{3,2,1,0:T(1,128)S(1)} all-to-all(f32[16,17,1,128]{3,2,1,0:T(1,128)S(1)} %sums_far.1), channel_id=1, replica_groups=mesh['far'=16,'near'=16] {'far'}, dimensions={0} | all-to-all | bytes 278528 | tf_op jit(solution)/shard_map/all_to_all | solution.py:298
  52.4 0.1 sums_near.1
  52.5 12.7 %all_to_all.17 = f32[16,17,1,128]{3,2,1,0:T(1,128)S(1)} all-to-all(f32[16,17,1,128]{3,2,1,0:T(1,128)S(1)} %sums_near.1), channel_id=1, replica_groups=mesh['far'=16,'near'=16] {'near'}, dimensions={0} | all-to-all | bytes 278528 | tf_op jit(solution)/shard_map/all_to_all | solution.py:298
  65.2 17.5 %finish.1 = f32[128,4096]{1,0:T(8,128)} custom-call(f32[272,128]{1,0:T(8,128)S(1)} %bitcast.3, bf16[256,4096]{1,0:T(8,128)(2,1)S(1)} %get-tuple-element.17.high_ref, bf16[256,4096]{1,0:T(8,128)(2,1)S(1)} %get-tuple-element.18.low_ref), custom_call_target="tpu_custom_call" | custom-call | tf_op jit(solution)/shard_map/finish/pallas_call | solution.py:371
Async XLA Ops:
  0.0 8.9 %copy-start.1 = (f32[128,4096]{1,0:T(8,128)S(1)}, f32[128,4096]{1,0:T(8,128)}, u32[]{:S(2)}) copy-start(f32[128,4096]{1,0:T(8,128)} %band_ref.3) | copy-start | bytes 6291460
  0.0 8.9 %copy-start.2 = (s32[128]{0:T(128)S(1)}, s32[128]{0:T(128)}, u32[]{:S(2)}) copy-start(s32[128]{0:T(128)} %param.5) | copy-start | bytes 1540
  2.0 10.5 %collective-permute-start = (f32[64,896]{1,0:T(8,128)}, f32[64,896]{1,0:T(8,128)S(1)}, u32[]{:S(2)}, u32[]{:S(2)}) collective-permute-start(f32[64,896]{1,0:T(8,128)} %get-tuple-element.12), channel_id=1, source_target_pairs={{0,1},{1,2},{2,3},{3,4},{4,5},{5,6},{6,7},{7,8},{8,9},{9,10},{10,1... | collective-permute-start | bytes 688136 | tf_op jit(solution)/shard_map/ppermute | solution.py:331
  6.9 7.5 %collective-permute-start.1 = (f32[64,896]{1,0:T(8,128)}, f32[64,896]{1,0:T(8,128)S(1)}, u32[]{:S(2)}, u32[]{:S(2)}) collective-permute-start(f32[64,896]{1,0:T(8,128)} %get-tuple-element.13), channel_id=1, source_target_pairs={{1,0},{2,1},{3,2},{4,3},{5,4},{6,5},{7,6},{8,7},{9,8},{10,9},{11,1... | collective-permute-start | bytes 688136 | tf_op jit(solution)/shard_map/ppermute | solution.py:332
  8.9 5.6 %copy-start = (f32[64,4096]{1,0:T(8,128)S(1)}, f32[64,4096]{1,0:T(8,128)}, u32[]{:S(2)}) copy-start(f32[64,4096]{1,0:T(8,128)} %src_ref.3) | copy-start | bytes 3145732

commit v6 on v5

--- a/solution.py
+++ b/solution.py
@@ -246,28 +246,29 @@
                 work[tile(g, t)] = rest[t]
 
 
-def compress(gram, spanning, work):
-    retain, order = spanning.shape
-    metric = exact(exact(spanning, gram), spanning, NT)
-    work[:, :retain] = 0.5 * (metric + metric.T)
-    work[:, retain : retain + order] = spanning
-    eliminate(work, (retain + order) // 128)
-    return work[:, retain : retain + order]
+def solve(metric, image, work):
+    order, width = image.shape
+    work[:, :order] = metric
+    work[:, order : order + width] = image
+    eliminate(work, (order + width) // 128)
+    return work[:, order : order + width]
 
 
 def finish_kernel(gram_ref, high_ref, low_ref, out_ref, work, out, sems):
     keep = out_ref.shape[0]
     g11, g12, g22 = unpack(gram_ref)
-    one = compress(g11, g11, work)
-    one = compress(g11, exact(one, g11), work)
+    square = exact(g11, g11)
+    span = solve(exact(square, g11, NT), square, work)
+    one = solve(exact(exact(span, g11), span, NT), span, work)
     cross = exact(exact(one, g12), one, NT)
     tail = exact(exact(one, g22), one, NT)
     same = jnp.where(places(keep) == 0, 1.0, 0.0)
     top = jnp.concatenate([same, cross], axis=1)
     bottom = jnp.concatenate([cross.T, tail], axis=1)
     gram = jnp.concatenate([top, bottom], axis=0)
-    two = compress(gram, exact(top, gram), work)
-    overall = jnp.concatenate([exact(two[:, :keep], one), exact(two[:, keep:], one)], axis=1)
+    span = exact(top, gram)
+    image = jnp.concatenate([exact(span[:, :keep], one), exact(span[:, keep:], one)], axis=1)
+    overall = solve(exact(exact(span, gram), span, NT), image, work)
     fh, fl = split(overall)
     both = jnp.concatenate([fh, fl], axis=0)
 
@@ -310,7 +311,7 @@
 
 def body(source, band_values, offsets):
     devices = lax.axis_size(ROWS)
-    group = lax.axis_size("near")
+    group = lax.axis_size("far")
     rows, width = source.shape
     reach = 3 * HB
     inner = width // WB
@@ -364,8 +365,8 @@
         name="powers",
     )(source, low, high, offsets, by_high, by_low)
 
-    gram = exchange(gram.reshape(group, -1, 1, 2 * rows), "near")
-    gram = summed_copies(summed_copies(gram, "far"), "near")
+    gram = exchange(gram.reshape(group, -1, 1, 2 * rows), "far")
+    gram = summed_copies(summed_copies(gram, "near"), "far")
     gram = gram.reshape(4 * rows + 16, 2 * rows)
 
     return pl.pallas_call(

time: 83.2 us -> 80.1 us (0.963)
  blocking collectives: 44.5 us -> 42 us
    all_to_all x3, blocking collectives: 44.5 us -> 42 us  [exchange(): return lax.all_to_all(blocks, axis, 0, 0, tiled=True)]
where the time goes in v6:
time: 80.1 us; the launch traced here: 79.8 us
  blocking collectives  42 us (52%)
  Pallas kernels  28.7 us (36%)
  starting transfers between devices  6.84 us (9%)
  waiting for transfers between devices  1.99 us (2%)
    all_to_all x3, blocking collectives, exchange(): return lax.all_to_all(blocks, axis, 0, 0, tiled=True)  42 us
    pallas_call x1, Pallas kernels, body(): pl.pallas_call(finish_kernel, out_shape=jax.ShapeDtypeStruct((2 * rows, w...  16.9 us
    pallas_call x1, Pallas kernels, body(): pl.pallas_call(functools.partial(powers_kernel, float(width * devices)),...  6.03 us
    ppermute x1, starting transfers between devices, body(): low = lax.ppermute(last, ROWS, up)  4.92 us
    pallas_call x1, Pallas kernels, body(): pl.pallas_call(blocks_kernel, out_shape=[blocks, blocks], scratch_shapes=...  3.58 us
    pallas_call x1, Pallas kernels, body(): pl.pallas_call(edges_kernel, out_shape=[edge, edge], in_specs=[hbm, hbm],...  1.99 us
    ppermute x1, waiting for transfers between devices, body(): high = lax.ppermute(first, ROWS, down)  1.99 us
    ppermute x1, starting transfers between devices, body(): high = lax.ppermute(first, ROWS, down)  1.92 us
  transfers between devices with their start and end apart: 2, of which 1 were waited for; matrix products, arithmetic and copies ran while one was open for 0% of the time, Pallas kernels for 4%

profile of v6, /device:TPU:1, one launch (start us, length us, event | category | flops | bytes accessed | tf_op | source)
XLA Modules:
  0.0 79.8 jit_solution(4037461445295029142)
XLA Ops:
  0.0 0.0 copy-start.1
  0.0 0.0 copy-start.2
  0.0 2.0 %edges.1 = (f32[64,896]{1,0:T(8,128)}, f32[64,896]{1,0:T(8,128)}) custom-call(f32[64,4096]{1,0:T(8,128)} %src_ref.3, f32[128,4096]{1,0:T(8,128)} %band_ref.3), custom_call_target="tpu_custom_call" | custom-call | tf_op jit(solution)/shard_map/edges/pallas_call | solution.py:324
  2.0 4.9 %collective-permute-start = (f32[64,896]{1,0:T(8,128)}, f32[64,896]{1,0:T(8,128)S(1)}, u32[]{:S(2)}, u32[]{:S(2)}) collective-permute-start(f32[64,896]{1,0:T(8,128)} %get-tuple-element.12), channel_id=1, source_target_pairs={{0,1},{1,2},{2,3},{3,4},{4,5},{5,6},{6,7},{7,8},{8,9},{9,10},{10,1... | collective-permute-start | bytes 688136 | tf_op jit(solution)/shard_map/ppermute | solution.py:332
  6.9 1.9 %collective-permute-start.1 = (f32[64,896]{1,0:T(8,128)}, f32[64,896]{1,0:T(8,128)S(1)}, u32[]{:S(2)}, u32[]{:S(2)}) collective-permute-start(f32[64,896]{1,0:T(8,128)} %get-tuple-element.13), channel_id=1, source_target_pairs={{1,0},{2,1},{3,2},{4,3},{5,4},{6,5},{7,6},{8,7},{9,8},{10,9},{11,1... | collective-permute-start | bytes 688136 | tf_op jit(solution)/shard_map/ppermute | solution.py:333
  8.9 0.0 copy-done.1
  8.9 0.0 copy-done.2
  8.9 0.0 copy-start
  8.9 3.6 %blocks.1 = (bf16[16,512,256]{2,1,0:T(8,128)(2,1)S(1)}, bf16[16,512,256]{2,1,0:T(8,128)(2,1)S(1)}) custom-call(f32[128,4096]{1,0:T(8,128)S(1)} %copy-done.1, s32[1,128]{1,0:T(1,128)S(1)} %bitcast.5), custom_call_target="tpu_custom_call" | custom-call | flops 10000000000 | bytes 12000000 | tf_op jit(solution)/shard_map/blocks/pallas_call | solution.py:336
  12.5 0.0 collective-permute-done.low_in
  12.5 2.0 %collective-permute-done.1.high_in = f32[64,896]{1,0:T(8,128)S(1)} collective-permute-done((f32[64,896]{1,0:T(8,128)}, f32[64,896]{1,0:T(8,128)S(1)}, u32[]{:S(2)}, u32[]{:S(2)}) %collective-permute-start.1) | collective-permute-done | bytes 229408 | tf_op jit(solution)/shard_map/ppermute | solution.py:333
  14.5 0.0 copy-done
  14.5 6.0 %powers.1 = (bf16[256,4096]{1,0:T(8,128)(2,1)S(1)}, bf16[256,4096]{1,0:T(8,128)(2,1)S(1)}, f32[272,128]{1,0:T(8,128)S(1)}) custom-call(f32[64,4096]{1,0:T(8,128)S(1)} %copy-done, f32[64,896]{1,0:T(8,128)S(1)} %collective-permute-done.low_in, f32[64,896]{1,0:T(8,128)S(1)} %collective-permute-done.1.high_in, s32[1,128]{1,0:T(1,128)S(1)} %bitcast.6, ...), custom_call_target="tpu_custom_call" | custom-call | tf_op jit(solution)/shard_map/powers/pallas_call | solution.py:351
  20.5 13.5 %all_to_all.15.in_ref = f32[16,17,1,128]{3,2,1,0:T(1,128)S(1)} all-to-all(f32[16,17,1,128]{3,2,1,0:T(1,128)S(1)} %bitcast.4), channel_id=1, replica_groups=mesh['far'=16,'near'=16] {'far'}, dimensions={0} | all-to-all | bytes 278528 | tf_op jit(solution)/shard_map/all_to_all | solution.py:299
  34.0 0.1 sums_near.1
  34.1 18.4 %all_to_all.16.in_ref = f32[16,17,1,128]{3,2,1,0:T(1,128)S(1)} all-to-all(f32[16,17,1,128]{3,2,1,0:T(1,128)S(1)} %sums_near.1), channel_id=1, replica_groups=mesh['far'=16,'near'=16] {'near'}, dimensions={0} | all-to-all | bytes 278528 | tf_op jit(solution)/shard_map/all_to_all | solution.py:299
  52.5 0.1 sums_far.1
  52.6 10.1 %all_to_all.17 = f32[16,17,1,128]{3,2,1,0:T(1,128)S(1)} all-to-all(f32[16,17,1,128]{3,2,1,0:T(1,128)S(1)} %sums_far.1), channel_id=1, replica_groups=mesh['far'=16,'near'=16] {'far'}, dimensions={0} | all-to-all | bytes 278528 | tf_op jit(solution)/shard_map/all_to_all | solution.py:299
  62.7 16.9 %finish.1 = f32[128,4096]{1,0:T(8,128)} custom-call(f32[272,128]{1,0:T(8,128)S(1)} %bitcast.3, bf16[256,4096]{1,0:T(8,128)(2,1)S(1)} %get-tuple-element.17.high_ref, bf16[256,4096]{1,0:T(8,128)(2,1)S(1)} %get-tuple-element.18.low_ref), custom_call_target="tpu_custom_call" | custom-call | tf_op jit(solution)/shard_map/finish/pallas_call | solution.py:372
Async XLA Ops:
  0.0 8.9 %copy-start.1 = (f32[128,4096]{1,0:T(8,128)S(1)}, f32[128,4096]{1,0:T(8,128)}, u32[]{:S(2)}) copy-start(f32[128,4096]{1,0:T(8,128)} %band_ref.3) | copy-start | bytes 6291460
  0.0 8.9 %copy-start.2 = (s32[128]{0:T(128)S(1)}, s32[128]{0:T(128)}, u32[]{:S(2)}) copy-start(s32[128]{0:T(128)} %param.5) | copy-start | bytes 1540
  2.0 10.5 %collective-permute-start = (f32[64,896]{1,0:T(8,128)}, f32[64,896]{1,0:T(8,128)S(1)}, u32[]{:S(2)}, u32[]{:S(2)}) collective-permute-start(f32[64,896]{1,0:T(8,128)} %get-tuple-element.12), channel_id=1, source_target_pairs={{0,1},{1,2},{2,3},{3,4},{4,5},{5,6},{6,7},{7,8},{8,9},{9,10},{10,1... | collective-permute-start | bytes 688136 | tf_op jit(solution)/shard_map/ppermute | solution.py:332
  6.9 7.5 %collective-permute-start.1 = (f32[64,896]{1,0:T(8,128)}, f32[64,896]{1,0:T(8,128)S(1)}, u32[]{:S(2)}, u32[]{:S(2)}) collective-permute-start(f32[64,896]{1,0:T(8,128)} %get-tuple-element.13), channel_id=1, source_target_pairs={{1,0},{2,1},{3,2},{4,3},{5,4},{6,5},{7,6},{8,7},{9,8},{10,9},{11,1... | collective-permute-start | bytes 688136 | tf_op jit(solution)/shard_map/ppermute | solution.py:333
  8.9 5.6 %copy-start = (f32[64,4096]{1,0:T(8,128)S(1)}, f32[64,4096]{1,0:T(8,128)}, u32[]{:S(2)}) copy-start(f32[64,4096]{1,0:T(8,128)} %src_ref.3) | copy-start | bytes 3145732

commit v7 on v6

--- a/solution.py
+++ b/solution.py
@@ -326,9 +326,9 @@
         out_shape=[edge, edge],
         in_specs=[hbm, hbm],
         scratch_shapes=[pltpu.SemaphoreType.DMA((6,))],
-        compiler_params=pltpu.CompilerParams(vmem_limit_bytes=64_500_000),
+        compiler_params=pltpu.CompilerParams(vmem_limit_bytes=4 * 1024 * 1024),
         name="edges",
-    )(source, band_values)
+    )(*[pltpu.with_memory_space_constraint(x, pltpu.HBM) for x in (source, band_values)])
     low = lax.ppermute(last, ROWS, up)
     high = lax.ppermute(first, ROWS, down)
     offsets = offsets.reshape(1, -1)

time: 80.1 us -> 79.1 us (0.988)
  transfers between devices with their start and end apart: 2 -> 2, of which waited for: 1 -> 1; matrix products, arithmetic and copies ran while one was open for 0% -> 0% of each run, Pallas kernels for 4% -> 5%
where the time goes in v7:
time: 79.1 us; the launch traced here: 78.9 us
  blocking collectives  42 us (53%)
  Pallas kernels  28 us (35%)
  starting transfers between devices  6.84 us (9%)
  waiting for transfers between devices  1.78 us (2%)
    all_to_all x3, blocking collectives, exchange(): return lax.all_to_all(blocks, axis, 0, 0, tiled=True)  42 us
    pallas_call x1, Pallas kernels, body(): pl.pallas_call(finish_kernel, out_shape=jax.ShapeDtypeStruct((2 * rows, w...  16.9 us
    pallas_call x1, Pallas kernels, body(): pl.pallas_call(functools.partial(powers_kernel, float(width * devices)),...  6.04 us
    ppermute x1, starting transfers between devices, body(): low = lax.ppermute(last, ROWS, up)  4.92 us
    pallas_call x1, Pallas kernels, body(): pl.pallas_call(blocks_kernel, out_shape=[blocks, blocks], scratch_shapes=...  3.58 us
    ppermute x1, starting transfers between devices, body(): high = lax.ppermute(first, ROWS, down)  1.92 us
    ppermute x1, waiting for transfers between devices, body(): high = lax.ppermute(first, ROWS, down)  1.78 us
  transfers between devices with their start and end apart: 2, of which 1 were waited for; matrix products, arithmetic and copies ran while one was open for 0% of the time, Pallas kernels for 5%

profile of v7, /device:TPU:1, one launch (start us, length us, event | category | flops | bytes accessed | tf_op | source)
XLA Modules:
  0.0 78.9 jit_solution(3012666972261536045)
XLA Ops:
  0.0 0.0 copy-start.1
  0.0 0.0 copy-start.2
  0.0 1.2 %edges.1 = (f32[64,896]{1,0:T(8,128)S(1)}, f32[64,896]{1,0:T(8,128)S(1)}) custom-call(f32[64,4096]{1,0:T(8,128)} %src_ref.3, f32[128,4096]{1,0:T(8,128)} %band_ref.3), custom_call_target="tpu_custom_call" | custom-call | tf_op jit(solution)/shard_map/edges/pallas_call | solution.py:324
  1.2 4.9 %collective-permute-start = (f32[64,896]{1,0:T(8,128)S(1)}, f32[64,896]{1,0:T(8,128)S(1)}, u32[]{:S(2)}, u32[]{:S(2)}) collective-permute-start(f32[64,896]{1,0:T(8,128)S(1)} %get-tuple-element.12), channel_id=1, source_target_pairs={{0,1},{1,2},{2,3},{3,4},{4,5},{5,6},{6,7},{7,8},{8,9},{9,10},{10,1... | collective-permute-start | bytes 688136 | tf_op jit(solution)/shard_map/ppermute | solution.py:332
  6.2 1.9 %collective-permute-start.1 = (f32[64,896]{1,0:T(8,128)S(1)}, f32[64,896]{1,0:T(8,128)S(1)}, u32[]{:S(2)}, u32[]{:S(2)}) collective-permute-start(f32[64,896]{1,0:T(8,128)S(1)} %get-tuple-element.13), channel_id=1, source_target_pairs={{1,0},{2,1},{3,2},{4,3},{5,4},{6,5},{7,6},{8,7},{9,8},{10,9},{11,1... | collective-permute-start | bytes 688136 | tf_op jit(solution)/shard_map/ppermute | solution.py:333
  8.1 0.0 copy-done.1
  8.1 0.0 copy-done.2
  8.1 0.0 copy-start
  8.1 3.6 %blocks.1 = (bf16[16,512,256]{2,1,0:T(8,128)(2,1)S(1)}, bf16[16,512,256]{2,1,0:T(8,128)(2,1)S(1)}) custom-call(f32[128,4096]{1,0:T(8,128)S(1)} %copy-done.1, s32[1,128]{1,0:T(1,128)S(1)} %bitcast.5), custom_call_target="tpu_custom_call" | custom-call | flops 10000000000 | bytes 12000000 | tf_op jit(solution)/shard_map/blocks/pallas_call | solution.py:336
  11.7 0.0 collective-permute-done.low_in
  11.7 1.8 %collective-permute-done.1.high_in = f32[64,896]{1,0:T(8,128)S(1)} collective-permute-done((f32[64,896]{1,0:T(8,128)S(1)}, f32[64,896]{1,0:T(8,128)S(1)}, u32[]{:S(2)}, u32[]{:S(2)}) %collective-permute-start.1) | collective-permute-done | bytes 229408 | tf_op jit(solution)/shard_map/ppermute | solution.py:333
  13.5 0.0 copy-done
  13.5 6.0 %powers.1 = (bf16[256,4096]{1,0:T(8,128)(2,1)S(1)}, bf16[256,4096]{1,0:T(8,128)(2,1)S(1)}, f32[272,128]{1,0:T(8,128)S(1)}) custom-call(f32[64,4096]{1,0:T(8,128)S(1)} %copy-done, f32[64,896]{1,0:T(8,128)S(1)} %collective-permute-done.low_in, f32[64,896]{1,0:T(8,128)S(1)} %collective-permute-done.1.high_in, s32[1,128]{1,0:T(1,128)S(1)} %bitcast.6, ...), custom_call_target="tpu_custom_call" | custom-call | tf_op jit(solution)/shard_map/powers/pallas_call | solution.py:351
  19.6 13.4 %all_to_all.15.in_ref = f32[16,17,1,128]{3,2,1,0:T(1,128)S(1)} all-to-all(f32[16,17,1,128]{3,2,1,0:T(1,128)S(1)} %bitcast.4), channel_id=1, replica_groups=mesh['far'=16,'near'=16] {'far'}, dimensions={0} | all-to-all | bytes 278528 | tf_op jit(solution)/shard_map/all_to_all | solution.py:299
  33.0 0.1 sums_near.1
  33.1 18.4 %all_to_all.16.in_ref = f32[16,17,1,128]{3,2,1,0:T(1,128)S(1)} all-to-all(f32[16,17,1,128]{3,2,1,0:T(1,128)S(1)} %sums_near.1), channel_id=1, replica_groups=mesh['far'=16,'near'=16] {'near'}, dimensions={0} | all-to-all | bytes 278528 | tf_op jit(solution)/shard_map/all_to_all | solution.py:299
  51.5 0.1 sums_far.1
  51.6 10.1 %all_to_all.17 = f32[16,17,1,128]{3,2,1,0:T(1,128)S(1)} all-to-all(f32[16,17,1,128]{3,2,1,0:T(1,128)S(1)} %sums_far.1), channel_id=1, replica_groups=mesh['far'=16,'near'=16] {'far'}, dimensions={0} | all-to-all | bytes 278528 | tf_op jit(solution)/shard_map/all_to_all | solution.py:299
  61.8 16.9 %finish.1 = f32[128,4096]{1,0:T(8,128)} custom-call(f32[272,128]{1,0:T(8,128)S(1)} %bitcast.3, bf16[256,4096]{1,0:T(8,128)(2,1)S(1)} %get-tuple-element.17.high_ref, bf16[256,4096]{1,0:T(8,128)(2,1)S(1)} %get-tuple-element.18.low_ref), custom_call_target="tpu_custom_call" | custom-call | tf_op jit(solution)/shard_map/finish/pallas_call | solution.py:372
Async XLA Ops:
  0.0 8.1 %copy-start.1 = (f32[128,4096]{1,0:T(8,128)S(1)}, f32[128,4096]{1,0:T(8,128)}, u32[]{:S(2)}) copy-start(f32[128,4096]{1,0:T(8,128)} %band_ref.3) | copy-start | bytes 6291460
  0.0 8.1 %copy-start.2 = (s32[128]{0:T(128)S(1)}, s32[128]{0:T(128)}, u32[]{:S(2)}) copy-start(s32[128]{0:T(128)} %param.5) | copy-start | bytes 1540
  1.2 10.5 %collective-permute-start = (f32[64,896]{1,0:T(8,128)S(1)}, f32[64,896]{1,0:T(8,128)S(1)}, u32[]{:S(2)}, u32[]{:S(2)}) collective-permute-start(f32[64,896]{1,0:T(8,128)S(1)} %get-tuple-element.12), channel_id=1, source_target_pairs={{0,1},{1,2},{2,3},{3,4},{4,5},{5,6},{6,7},{7,8},{8,9},{9,10},{10,1... | collective-permute-start | bytes 688136 | tf_op jit(solution)/shard_map/ppermute | solution.py:332
  6.2 7.3 %collective-permute-start.1 = (f32[64,896]{1,0:T(8,128)S(1)}, f32[64,896]{1,0:T(8,128)S(1)}, u32[]{:S(2)}, u32[]{:S(2)}) collective-permute-start(f32[64,896]{1,0:T(8,128)S(1)} %get-tuple-element.13), channel_id=1, source_target_pairs={{1,0},{2,1},{3,2},{4,3},{5,4},{6,5},{7,6},{8,7},{9,8},{10,9},{11,1... | collective-permute-start | bytes 688136 | tf_op jit(solution)/shard_map/ppermute | solution.py:333
  8.1 5.4 %copy-start = (f32[64,4096]{1,0:T(8,128)S(1)}, f32[64,4096]{1,0:T(8,128)}, u32[]{:S(2)}) copy-start(f32[64,4096]{1,0:T(8,128)} %src_ref.3) | copy-start | bytes 3145732

commit v8 on v7

--- a/solution.py
+++ b/solution.py
@@ -80,11 +80,19 @@
     return jnp.sum(values * last, axis=0, keepdims=True)
 
 
-def blocks_kernel(band_ref, off_ref, wh, wl, both_ref, diag_ref, rolled_ref):
+def blocks_kernel(
+    band_ref, off_ref, src_ref, wh, wl, s_ref, a_ref, both_ref, diag_ref, rolled_ref
+):
     pick, last = picker(off_ref)
     count = wh.shape[0]
+    rows = src_ref.shape[0]
     for b in range(count + 3):
-        if b >= 3:
+        if 5 <= b:
+            k = b - 4
+            pair = applied(s_ref[:, k * WB - HB : k * WB - HB + SPAN], wh[k], wl[k])
+            for part in range(2):
+                a_ref[part * rows : (part + 1) * rows, k * WB : k * WB + WB] = pair[part]
+        if 3 <= b:
             values = band_ref[:, (b - 3) * WB : (b - 2) * WB]
             place_block(rolled_ref[(b - 3) % 2], final(values, last), wh, wl, b - 3)
         if 2 <= b < count + 2:
@@ -92,7 +100,15 @@
         if 1 <= b < count + 1:
             diag_ref[(b - 1) % 2] = mm(both_ref[(b - 1) % 2], pick, NT)
         if b < count:
-            both_ref[b % 2] = turned(band_ref[:, b * WB : b * WB + WB])
+            at = slice(b * WB, b * WB + WB)
+            both_ref[b % 2] = turned(band_ref[:, at])
+            s_ref[:rows, at], s_ref[rows:, at] = split(src_ref[:, at])
+
+
+def applied(window, by_high, by_low):
+    rows = window.shape[0] // 2
+    both = mm(window, by_high)
+    return split(both[:rows] + both[rows:] + mm(window[:rows], by_low))
 
 
 def edges_kernel(src_ref, band_ref, up_ref, down_ref, sems):
@@ -113,20 +129,18 @@
 
 
 def powers_kernel(
-    total, src_ref, low_in, high_in, off_ref, wh, wl, high_ref, low_ref, gram_ref, xs, eh, el, rolled
+    total, s_ref, a_ref, low_in, high_in, off_ref, wh, wl, high_ref, low_ref, gram_ref, xs, eh, el, rolled
 ):
-    rows, width = src_ref.shape
+    rows, width = s_ref.shape[0] // 2, s_ref.shape[1]
     inner = width // WB
     reach = 3 * HB
     edges = [(low_in, 0, 0), (high_in, 1, reach + width)]
     for b in range(inner):
         at = slice(b * WB, b * WB + WB)
         into = slice(b * WB + reach, b * WB + reach + WB)
-        high, low = split(src_ref[:, at])
-        high_ref[:rows, at] = high
-        low_ref[:rows, at] = low
-        xs[0, :rows, into] = high
-        xs[0, rows:, into] = low
+        high_ref[:rows, at] = s_ref[:rows, at]
+        low_ref[:rows, at] = s_ref[rows:, at]
+        xs[0, :, into] = s_ref[:, at]
     pick, last = picker(off_ref)
     sides = []
     for ref, side, at in edges:
@@ -143,11 +157,6 @@
         for at in (0, xs.shape[2] - HB):
             xs[power, :, at : at + HB] = jnp.zeros((2 * rows, HB), jnp.bfloat16)
 
-    def apply(power, at, by_high, by_low):
-        window = xs[power - 1, :, at : at + SPAN]
-        both = mm(window, by_high)
-        return split(both[:rows] + both[rows:] + mm(window[:rows], by_low))
-
     for power in (1, 2, 3):
         inside = list(range(2, inner)) + [1, inner]
         for b in inside + [0, inner + 1] * (power < 3):
@@ -155,7 +164,11 @@
                 by = (eh[int(b > 0)], el[int(b > 0)])
             else:
                 by = (wh[b - 1], wl[b - 1])
-            pair = apply(power, b * WB, *by)
+            if power == 1 and 1 < b < inner:
+                at = slice(b * WB - WB, b * WB)
+                pair = a_ref[:rows, at], a_ref[rows:, at]
+            else:
+                pair = applied(xs[power - 1, :, b * WB : b * WB + SPAN], *by)
             if power < 3:
                 for part in range(2):
                     place = slice(b * WB + HB, b * WB + HB + WB)
@@ -333,9 +346,10 @@
     high = lax.ppermute(first, ROWS, down)
     offsets = offsets.reshape(1, -1)
     blocks = jax.ShapeDtypeStruct((inner, SPAN, WB), jnp.bfloat16)
-    by_high, by_low = pl.pallas_call(
+    stacked = jax.ShapeDtypeStruct((2 * rows, width), jnp.bfloat16)
+    by_high, by_low, inside, once = pl.pallas_call(
         blocks_kernel,
-        out_shape=[blocks, blocks],
+        out_shape=[blocks, blocks, stacked, stacked],
         scratch_shapes=[
             pltpu.VMEM((2, WB, 2 * HB), jnp.bfloat16),
             pltpu.VMEM((2, WB, 2 * HB), jnp.float32),
@@ -346,7 +360,7 @@
             flops=10_000_000_000, bytes_accessed=12_000_000, transcendentals=0
         ),
         name="blocks",
-    )(band_values, offsets)
+    )(band_values, offsets, source)
     wide = width + 2 * reach
     high, low, gram = pl.pallas_call(
         functools.partial(powers_kernel, float(width * devices)),
@@ -363,7 +377,7 @@
         ],
         compiler_params=pltpu.CompilerParams(vmem_limit_bytes=16 * 1024 * 1024),
         name="powers",
-    )(source, low, high, offsets, by_high, by_low)
+    )(inside, once, low, high, offsets, by_high, by_low)
 
     gram = exchange(gram.reshape(group, -1, 1, 2 * rows), "far")
     gram = summed_copies(summed_copies(gram, "near"), "far")

time: 79.1 us -> 78.8 us (level)
  waiting for transfers between devices: 1.78 us -> 0.82 us
  blocking collectives: 42 us -> 42.9 us
    pallas_call x1, Pallas kernels: 6.04 us -> 4.8 us  [body(): pl.pallas_call(functools.partial(powers_kernel, float(width * devices)),...]
    pallas_call x1, Pallas kernels: 3.58 us -> 4.54 us  [body(): pl.pallas_call(blocks_kernel, out_shape=[blocks, blocks, stacked, stacked...]
    ppermute x1, waiting for transfers between devices: 1.78 us -> 0.82 us  [body(): high = lax.ppermute(first, ROWS, down)]
    all_to_all x3, blocking collectives: 42 us -> 42.9 us  [exchange(): return lax.all_to_all(blocks, axis, 0, 0, tiled=True)]
  transfers between devices with their start and end apart: 2 -> 2, of which waited for: 1 -> 1; matrix products, arithmetic and copies ran while one was open for 0% -> 0% of each run, Pallas kernels for 5% -> 6%
where the time goes in v8:
time: 78.8 us; the launch traced here: 78.6 us
  blocking collectives  42.9 us (54%)
  Pallas kernels  27.7 us (35%)
  starting transfers between devices  6.84 us (9%)
  waiting for transfers between devices  0.82 us (1%)
    all_to_all x3, blocking collectives, exchange(): return lax.all_to_all(blocks, axis, 0, 0, tiled=True)  42.9 us
    pallas_call x1, Pallas kernels, body(): pl.pallas_call(finish_kernel, out_shape=jax.ShapeDtypeStruct((2 * rows, w...  16.9 us
    ppermute x1, starting transfers between devices, body(): low = lax.ppermute(last, ROWS, up)  4.92 us
    pallas_call x1, Pallas kernels, body(): pl.pallas_call(functools.partial(powers_kernel, float(width * devices)),...  4.8 us
    pallas_call x1, Pallas kernels, body(): pl.pallas_call(blocks_kernel, out_shape=[blocks, blocks, stacked, stacked...  4.54 us
    ppermute x1, starting transfers between devices, body(): high = lax.ppermute(first, ROWS, down)  1.92 us
  transfers between devices with their start and end apart: 2, of which 1 were waited for; matrix products, arithmetic and copies ran while one was open for 0% of the time, Pallas kernels for 6%

profile of v8, /device:TPU:1, one launch (start us, length us, event | category | flops | bytes accessed | tf_op | source)
XLA Modules:
  0.0 78.6 jit_solution(14933859610372111974)
XLA Ops:
  0.0 0.0 copy-start
  0.0 0.0 copy-start.1
  0.0 0.0 copy-start.2
  0.0 1.2 %edges.1 = (f32[64,896]{1,0:T(8,128)S(1)}, f32[64,896]{1,0:T(8,128)S(1)}) custom-call(f32[64,4096]{1,0:T(8,128)} %src_ref.3, f32[128,4096]{1,0:T(8,128)} %band_ref.3), custom_call_target="tpu_custom_call" | custom-call | tf_op jit(solution)/shard_map/edges/pallas_call | solution.py:337
  1.3 4.9 %collective-permute-start = (f32[64,896]{1,0:T(8,128)S(1)}, f32[64,896]{1,0:T(8,128)S(1)}, u32[]{:S(2)}, u32[]{:S(2)}) collective-permute-start(f32[64,896]{1,0:T(8,128)S(1)} %get-tuple-element.16), channel_id=1, source_target_pairs={{0,1},{1,2},{2,3},{3,4},{4,5},{5,6},{6,7},{7,8},{8,9},{9,10},{10,1... | collective-permute-start | bytes 688136 | tf_op jit(solution)/shard_map/ppermute | solution.py:345
  6.2 1.9 %collective-permute-start.1 = (f32[64,896]{1,0:T(8,128)S(1)}, f32[64,896]{1,0:T(8,128)S(1)}, u32[]{:S(2)}, u32[]{:S(2)}) collective-permute-start(f32[64,896]{1,0:T(8,128)S(1)} %get-tuple-element.17), channel_id=1, source_target_pairs={{1,0},{2,1},{3,2},{4,3},{5,4},{6,5},{7,6},{8,7},{9,8},{10,9},{11,1... | collective-permute-start | bytes 688136 | tf_op jit(solution)/shard_map/ppermute | solution.py:346
  8.1 0.0 copy-done
  8.1 0.0 copy-done.1
  8.1 0.0 copy-done.2
  8.1 4.5 %blocks.1 = (bf16[16,512,256]{2,1,0:T(8,128)(2,1)S(1)}, bf16[16,512,256]{2,1,0:T(8,128)(2,1)S(1)}, bf16[128,4096]{1,0:T(8,128)(2,1)S(1)}, bf16[128,4096]{1,0:T(8,128)(2,1)S(1)}) custom-call(f32[128,4096]{1,0:T(8,128)S(1)} %copy-done, s32[1,128]{1,0:T(1,128)S(1)} %bitcast.5, f32[64,4096]{1,0:T(8,128)S(1)} %copy-done.1), custom_call_target="tpu_custom_call" | custom-call | flops 10000000000 | bytes 12000000 | tf_op jit(solution)/shard_map/blocks/pallas_call | solution.py:350
  12.7 0.0 collective-permute-done.low_in
  12.7 0.8 %collective-permute-done.1.high_in = f32[64,896]{1,0:T(8,128)S(1)} collective-permute-done((f32[64,896]{1,0:T(8,128)S(1)}, f32[64,896]{1,0:T(8,128)S(1)}, u32[]{:S(2)}, u32[]{:S(2)}) %collective-permute-start.1) | collective-permute-done | bytes 229408 | tf_op jit(solution)/shard_map/ppermute | solution.py:346
  13.5 4.8 %powers.1 = (bf16[256,4096]{1,0:T(8,128)(2,1)S(1)}, bf16[256,4096]{1,0:T(8,128)(2,1)S(1)}, f32[272,128]{1,0:T(8,128)S(1)}) custom-call(bf16[128,4096]{1,0:T(8,128)(2,1)S(1)} %get-tuple-element.14.s_ref, bf16[128,4096]{1,0:T(8,128)(2,1)S(1)} %get-tuple-element.15.a_ref, f32[64,896]{1,0:T(8,128)S(1)} %collective-permute-done.low_in, ...), custom_call_target="tpu_custom_call" | custom-call | tf_op jit(solution)/shard_map/powers/pallas_call | solution.py:365
  18.3 13.4 %all_to_all.15.in_ref = f32[16,17,1,128]{3,2,1,0:T(1,128)S(1)} all-to-all(f32[16,17,1,128]{3,2,1,0:T(1,128)S(1)} %bitcast.4), channel_id=1, replica_groups=mesh['far'=16,'near'=16] {'far'}, dimensions={0} | all-to-all | bytes 278528 | tf_op jit(solution)/shard_map/all_to_all | solution.py:312
  31.8 0.1 sums_near.1
  31.9 19.4 %all_to_all.16.in_ref = f32[16,17,1,128]{3,2,1,0:T(1,128)S(1)} all-to-all(f32[16,17,1,128]{3,2,1,0:T(1,128)S(1)} %sums_near.1), channel_id=1, replica_groups=mesh['far'=16,'near'=16] {'near'}, dimensions={0} | all-to-all | bytes 278528 | tf_op jit(solution)/shard_map/all_to_all | solution.py:312
  51.3 0.1 sums_far.1
  51.4 10.1 %all_to_all.17 = f32[16,17,1,128]{3,2,1,0:T(1,128)S(1)} all-to-all(f32[16,17,1,128]{3,2,1,0:T(1,128)S(1)} %sums_far.1), channel_id=1, replica_groups=mesh['far'=16,'near'=16] {'far'}, dimensions={0} | all-to-all | bytes 278528 | tf_op jit(solution)/shard_map/all_to_all | solution.py:312
  61.5 16.9 %finish.1 = f32[128,4096]{1,0:T(8,128)} custom-call(f32[272,128]{1,0:T(8,128)S(1)} %bitcast.3, bf16[256,4096]{1,0:T(8,128)(2,1)S(1)} %get-tuple-element.21.high_ref, bf16[256,4096]{1,0:T(8,128)(2,1)S(1)} %get-tuple-element.22.low_ref), custom_call_target="tpu_custom_call" | custom-call | tf_op jit(solution)/shard_map/finish/pallas_call | solution.py:386
Async XLA Ops:
  0.0 8.1 %copy-start = (f32[128,4096]{1,0:T(8,128)S(1)}, f32[128,4096]{1,0:T(8,128)}, u32[]{:S(2)}) copy-start(f32[128,4096]{1,0:T(8,128)} %band_ref.3) | copy-start | bytes 6291460
  0.0 8.1 %copy-start.1 = (f32[64,4096]{1,0:T(8,128)S(1)}, f32[64,4096]{1,0:T(8,128)}, u32[]{:S(2)}) copy-start(f32[64,4096]{1,0:T(8,128)} %src_ref.3) | copy-start | bytes 3145732
  0.0 8.1 %copy-start.2 = (s32[128]{0:T(128)S(1)}, s32[128]{0:T(128)}, u32[]{:S(2)}) copy-start(s32[128]{0:T(128)} %param.5) | copy-start | bytes 1540
  1.3 11.4 %collective-permute-start = (f32[64,896]{1,0:T(8,128)S(1)}, f32[64,896]{1,0:T(8,128)S(1)}, u32[]{:S(2)}, u32[]{:S(2)}) collective-permute-start(f32[64,896]{1,0:T(8,128)S(1)} %get-tuple-element.16), channel_id=1, source_target_pairs={{0,1},{1,2},{2,3},{3,4},{4,5},{5,6},{6,7},{7,8},{8,9},{9,10},{10,1... | collective-permute-start | bytes 688136 | tf_op jit(solution)/shard_map/ppermute | solution.py:345
  6.2 7.3 %collective-permute-start.1 = (f32[64,896]{1,0:T(8,128)S(1)}, f32[64,896]{1,0:T(8,128)S(1)}, u32[]{:S(2)}, u32[]{:S(2)}) collective-permute-start(f32[64,896]{1,0:T(8,128)S(1)} %get-tuple-element.17), channel_id=1, source_target_pairs={{1,0},{2,1},{3,2},{4,3},{5,4},{6,5},{7,6},{8,7},{9,8},{10,9},{11,1... | collective-permute-start | bytes 688136 | tf_op jit(solution)/shard_map/ppermute | solution.py:346

commit v9 on v8

--- a/solution.py
+++ b/solution.py
@@ -245,9 +245,9 @@
             cross.append(crossing)
             tops.append(top)
         scale = lax.rsqrt(pivots)
-        for t in range(1, tiles):
+        for t in range(tiles):
             work[tile(kb, t)] = own[t] * scale
-        for g in range(kb + 1, order // 8):
+        for g in range(kb + 1, min(8 * (kb // 8) + 8 + 0, order // 8)):
             rest = [work[tile(g, t)] for t in range(tiles)]
             q = [lane_copy(rest[0], 8 * kb + j) for j in range(8)]
             for k in range(8):
@@ -257,6 +257,12 @@
                 rest = [x - m * y for x, y in zip(rest, tops[k])]
             for t in range(tiles):
                 work[tile(g, t)] = rest[t]
+        done = 8 * kb + 8
+        start = done + 8 * 0
+        if done % 64 == 0 and start < order:
+            panel = work[done - 64 : done, :]
+            rest = exact(panel[:, start:order], panel, (((0,), (0,)), ((), ())))
+            work[start:order, :] = work[start:order, :] - rest
 
 
 def solve(metric, image, work):

time: 78.8 us -> 77.6 us (0.985)
  Pallas kernels: 27.7 us -> 26.5 us
    pallas_call x1, Pallas kernels: 16.9 us -> 15.7 us  [body(): pl.pallas_call(finish_kernel, out_shape=jax.ShapeDtypeStruct((2 * rows, w...]
where the time goes in v9:
time: 77.6 us; the launch traced here: 77.3 us
  blocking collectives  42.9 us (55%)
  Pallas kernels  26.5 us (34%)
  starting transfers between devices  6.84 us (9%)
  waiting for transfers between devices  0.82 us (1%)
    all_to_all x3, blocking collectives, exchange(): return lax.all_to_all(blocks, axis, 0, 0, tiled=True)  42.9 us
    pallas_call x1, Pallas kernels, body(): pl.pallas_call(finish_kernel, out_shape=jax.ShapeDtypeStruct((2 * rows, w...  15.7 us
    ppermute x1, starting transfers between devices, body(): low = lax.ppermute(last, ROWS, up)  4.92 us
    pallas_call x1, Pallas kernels, body(): pl.pallas_call(functools.partial(powers_kernel, float(width * devices)),...  4.8 us
    pallas_call x1, Pallas kernels, body(): pl.pallas_call(blocks_kernel, out_shape=[blocks, blocks, stacked, stacked...  4.54 us
    ppermute x1, starting transfers between devices, body(): high = lax.ppermute(first, ROWS, down)  1.92 us
  transfers between devices with their start and end apart: 2, of which 1 were waited for; matrix products, arithmetic and copies ran while one was open for 0% of the time, Pallas kernels for 6%

profile of v9, /device:TPU:1, one launch (start us, length us, event | category | flops | bytes accessed | tf_op | source)
XLA Modules:
  0.0 77.3 jit_solution(3693056835422775146)
XLA Ops:
  0.0 0.0 copy-start
  0.0 0.0 copy-start.1
  0.0 0.0 copy-start.2
  0.0 1.2 %edges.1 = (f32[64,896]{1,0:T(8,128)S(1)}, f32[64,896]{1,0:T(8,128)S(1)}) custom-call(f32[64,4096]{1,0:T(8,128)} %src_ref.3, f32[128,4096]{1,0:T(8,128)} %band_ref.3), custom_call_target="tpu_custom_call" | custom-call | tf_op jit(solution)/shard_map/edges/pallas_call | solution.py:343
  1.3 4.9 %collective-permute-start = (f32[64,896]{1,0:T(8,128)S(1)}, f32[64,896]{1,0:T(8,128)S(1)}, u32[]{:S(2)}, u32[]{:S(2)}) collective-permute-start(f32[64,896]{1,0:T(8,128)S(1)} %get-tuple-element.16), channel_id=1, source_target_pairs={{0,1},{1,2},{2,3},{3,4},{4,5},{5,6},{6,7},{7,8},{8,9},{9,10},{10,1... | collective-permute-start | bytes 688136 | tf_op jit(solution)/shard_map/ppermute | solution.py:351
  6.2 1.9 %collective-permute-start.1 = (f32[64,896]{1,0:T(8,128)S(1)}, f32[64,896]{1,0:T(8,128)S(1)}, u32[]{:S(2)}, u32[]{:S(2)}) collective-permute-start(f32[64,896]{1,0:T(8,128)S(1)} %get-tuple-element.17), channel_id=1, source_target_pairs={{1,0},{2,1},{3,2},{4,3},{5,4},{6,5},{7,6},{8,7},{9,8},{10,9},{11,1... | collective-permute-start | bytes 688136 | tf_op jit(solution)/shard_map/ppermute | solution.py:352
  8.1 0.0 copy-done
  8.1 0.0 copy-done.1
  8.1 0.0 copy-done.2
  8.1 4.5 %blocks.1 = (bf16[16,512,256]{2,1,0:T(8,128)(2,1)S(1)}, bf16[16,512,256]{2,1,0:T(8,128)(2,1)S(1)}, bf16[128,4096]{1,0:T(8,128)(2,1)S(1)}, bf16[128,4096]{1,0:T(8,128)(2,1)S(1)}) custom-call(f32[128,4096]{1,0:T(8,128)S(1)} %copy-done, s32[1,128]{1,0:T(1,128)S(1)} %bitcast.5, f32[64,4096]{1,0:T(8,128)S(1)} %copy-done.1), custom_call_target="tpu_custom_call" | custom-call | flops 10000000000 | bytes 12000000 | tf_op jit(solution)/shard_map/blocks/pallas_call | solution.py:356
  12.7 0.0 collective-permute-done.low_in
  12.7 0.8 %collective-permute-done.1.high_in = f32[64,896]{1,0:T(8,128)S(1)} collective-permute-done((f32[64,896]{1,0:T(8,128)S(1)}, f32[64,896]{1,0:T(8,128)S(1)}, u32[]{:S(2)}, u32[]{:S(2)}) %collective-permute-start.1) | collective-permute-done | bytes 229408 | tf_op jit(solution)/shard_map/ppermute | solution.py:352
  13.5 4.8 %powers.1 = (bf16[256,4096]{1,0:T(8,128)(2,1)S(1)}, bf16[256,4096]{1,0:T(8,128)(2,1)S(1)}, f32[272,128]{1,0:T(8,128)S(1)}) custom-call(bf16[128,4096]{1,0:T(8,128)(2,1)S(1)} %get-tuple-element.14.s_ref, bf16[128,4096]{1,0:T(8,128)(2,1)S(1)} %get-tuple-element.15.a_ref, f32[64,896]{1,0:T(8,128)S(1)} %collective-permute-done.low_in, ...), custom_call_target="tpu_custom_call" | custom-call | tf_op jit(solution)/shard_map/powers/pallas_call | solution.py:371
  18.3 13.4 %all_to_all.15.in_ref = f32[16,17,1,128]{3,2,1,0:T(1,128)S(1)} all-to-all(f32[16,17,1,128]{3,2,1,0:T(1,128)S(1)} %bitcast.4), channel_id=1, replica_groups=mesh['far'=16,'near'=16] {'far'}, dimensions={0} | all-to-all | bytes 278528 | tf_op jit(solution)/shard_map/all_to_all | solution.py:318
  31.8 0.1 sums_near.1
  31.9 19.4 %all_to_all.16.in_ref = f32[16,17,1,128]{3,2,1,0:T(1,128)S(1)} all-to-all(f32[16,17,1,128]{3,2,1,0:T(1,128)S(1)} %sums_near.1), channel_id=1, replica_groups=mesh['far'=16,'near'=16] {'near'}, dimensions={0} | all-to-all | bytes 278528 | tf_op jit(solution)/shard_map/all_to_all | solution.py:318
  51.3 0.1 sums_far.1
  51.4 10.1 %all_to_all.17 = f32[16,17,1,128]{3,2,1,0:T(1,128)S(1)} all-to-all(f32[16,17,1,128]{3,2,1,0:T(1,128)S(1)} %sums_far.1), channel_id=1, replica_groups=mesh['far'=16,'near'=16] {'far'}, dimensions={0} | all-to-all | bytes 278528 | tf_op jit(solution)/shard_map/all_to_all | solution.py:318
  61.5 15.7 %finish.1 = f32[128,4096]{1,0:T(8,128)} custom-call(f32[272,128]{1,0:T(8,128)S(1)} %bitcast.3, bf16[256,4096]{1,0:T(8,128)(2,1)S(1)} %get-tuple-element.21.high_ref, bf16[256,4096]{1,0:T(8,128)(2,1)S(1)} %get-tuple-element.22.low_ref), custom_call_target="tpu_custom_call" | custom-call | tf_op jit(solution)/shard_map/finish/pallas_call | solution.py:392
Async XLA Ops:
  0.0 8.1 %copy-start = (f32[128,4096]{1,0:T(8,128)S(1)}, f32[128,4096]{1,0:T(8,128)}, u32[]{:S(2)}) copy-start(f32[128,4096]{1,0:T(8,128)} %band_ref.3) | copy-start | bytes 6291460
  0.0 8.1 %copy-start.1 = (f32[64,4096]{1,0:T(8,128)S(1)}, f32[64,4096]{1,0:T(8,128)}, u32[]{:S(2)}) copy-start(f32[64,4096]{1,0:T(8,128)} %src_ref.3) | copy-start | bytes 3145732
  0.0 8.1 %copy-start.2 = (s32[128]{0:T(128)S(1)}, s32[128]{0:T(128)}, u32[]{:S(2)}) copy-start(s32[128]{0:T(128)} %param.5) | copy-start | bytes 1540
  1.3 11.4 %collective-permute-start = (f32[64,896]{1,0:T(8,128)S(1)}, f32[64,896]{1,0:T(8,128)S(1)}, u32[]{:S(2)}, u32[]{:S(2)}) collective-permute-start(f32[64,896]{1,0:T(8,128)S(1)} %get-tuple-element.16), channel_id=1, source_target_pairs={{0,1},{1,2},{2,3},{3,4},{4,5},{5,6},{6,7},{7,8},{8,9},{9,10},{10,1... | collective-permute-start | bytes 688136 | tf_op jit(solution)/shard_map/ppermute | solution.py:351
  6.2 7.3 %collective-permute-start.1 = (f32[64,896]{1,0:T(8,128)S(1)}, f32[64,896]{1,0:T(8,128)S(1)}, u32[]{:S(2)}, u32[]{:S(2)}) collective-permute-start(f32[64,896]{1,0:T(8,128)S(1)} %get-tuple-element.17), channel_id=1, source_target_pairs={{1,0},{2,1},{3,2},{4,3},{5,4},{6,5},{7,6},{8,7},{9,8},{10,9},{11,1... | collective-permute-start | bytes 688136 | tf_op jit(solution)/shard_map/ppermute | solution.py:352
